TPU v7x, 32 devices: a whole 2x2x4 slice. The times are simulated.
32 devices in a mesh: shots: 2 (over x), mx: 16 (over z, y, core).
Axes of the slice: x: 2, y: 2, z: 4, core: 2. Of those that a mesh axis runs over, the one named last changes fastest.
Arguments:
- initial: float32 [18, 125, 2048], P('shots', None, 'mx'), parts along dimension 0, may hold values from -6 to 6
- derivative: float32 [3, 125, 125], replicated, may hold values from -0.5 to 0.5
- coupling: float32 [3, 9, 9], replicated, may hold values from -2 to 2
- face_lift: float32 [2, 125, 125], replicated, may hold values from -0.5 to 0.5
- metric: float32 [3, 2048], P(None, 'mx'), may hold values from 0.3 to 3
- rec_element: int32 [4096], P('mx'), may hold values from 0 to 127
- rec_weight: float32 [125, 4096], P(None, 'mx'), may hold values from -0.5 to 0.5
- live_counts: int32 [16], replicated, may hold values from 1 to 256, 2048 in all
- shot_order: int32 [4096], replicated, may hold values from 0 to 4095, as said below
- observed: float32 [8192, 48], P(('shots', 'mx')), parts along dimension 0, may hold values from -6 to 6
Outputs:
- residual: float32 [8192, 48], P(('shots', 'mx')), parts along dimension 0
- misfit: float32 [8192], P(('shots', 'mx')), parts along dimension 0
- adjoint: float32 [8192, 48], P(('shots', 'mx')), parts along dimension 0
There are 2 independent parts, one for each index of `shots`. A program takes and returns all parts, laid end to end along the dimension named above; an argument that names none is the same for every part. Nothing has to cross between parts.
Inputs may be any that keep to these rules, and one draw needn't show every extreme that they name: `rec_element`: local element index of the slot within its block of 128 elements. The live receivers of block b are its first live_counts[b] slots. `shot_order`: a permutation of the slots; of the 256 positions of each block of shot-receiver order, exactly 16 come from the slots of each block.
All inputs are finite; a program needn't handle non-finite values.
Results may differ from a plain program's by a relative error of at most 0.00018.
Values sent between devices are 32-bit elements; how exact they have to be, the bound alone decides.
A program may use at most 64 MiB of HBM per device.

v0:
```python
import functools
import jax
import jax.numpy as jnp
from jax import lax
from jax.experimental import pallas as pl
from jax.experimental.pallas import tpu as pltpu
from jax.sharding import PartitionSpec as P

STEPS = 12
COMPS = 4
HALO = 16
GUARD = 8


def split(x):
    hi = x.astype(jnp.bfloat16)
    return hi, (x - hi.astype(jnp.float32)).astype(jnp.bfloat16)


def zeros(*shape):
    return jnp.zeros(shape, jnp.float32)


def ones_where(cond):
    return jnp.where(cond, 1.0, 0.0).astype(jnp.bfloat16)


def dot(a, b):
    return jnp.dot(a, b, preferred_element_type=jnp.float32)


def permute(onehot, x):
    hi = x.astype(jnp.bfloat16)
    rest = x - hi.astype(jnp.float32)
    mid = rest.astype(jnp.bfloat16)
    low = (rest - mid.astype(jnp.float32)).astype(jnp.bfloat16)
    return dot(onehot, hi) + (dot(onehot, mid) + dot(onehot, low))


def greet(peers, me):
    barrier = pltpu.get_barrier_semaphore()

    def one(off, _):
        pl.semaphore_signal(barrier, inc=1, device_id={"mx": lax.rem(me + off, peers)}, device_id_type=pl.DeviceIdType.MESH)
        return 0

    lax.fori_loop(1, peers, one, 0)
    return barrier


def start_kernel(peers, initial, metric, derivative, face_lift, weight_in, order, counts,
                 state, wb, ws, to_send, from_send, to_place, from_place, live,
                 pad, padw, send_sem, recv_sem):
    fields, nodes, count = initial.shape
    lanes = pad.shape[0]
    slots = order.shape[1]
    pair = slots // peers
    me = lax.axis_index("mx")
    right, left = lax.rem(me + 1, peers), lax.rem(me + peers - 1, peers)
    barrier = pltpu.get_barrier_semaphore()
    for side in (left, right):
        pl.semaphore_signal(barrier, inc=1, device_id={"mx": side}, device_id_type=pl.DeviceIdType.MESH)
    pad[...] = zeros(lanes, lanes)
    for f in range(fields):
        pad[0:nodes, :] = initial[f]
        state[f, HALO:HALO + count] = pad[...].T
    kinds = metric.shape[0]
    for k in range(kinds):
        state[fields + k, HALO:HALO + count] = jnp.broadcast_to(metric[k:k + 1, :], (lanes, count)).T
    pl.semaphore_wait(barrier, 2)
    moved = fields + kinds
    copies = []
    for i, (side, at, to) in enumerate(((right, count, 0), (left, HALO, HALO + count))):
        copies.append(pltpu.make_async_remote_copy(
            src_ref=state.at[0:moved, at:at + HALO], dst_ref=state.at[0:moved, to:to + HALO],
            send_sem=send_sem.at[i], recv_sem=recv_sem.at[i],
            device_id={"mx": side}, device_id_type=pl.DeviceIdType.MESH))
        copies[-1].start()
    pad[...] = zeros(lanes, lanes)
    turns = derivative.shape[0]
    kdim = (turns + face_lift.shape[0]) * lanes
    for k in range(kdim // lanes):
        pad[0:nodes, 0:nodes] = derivative[k] if k < turns else face_lift[k - turns]
        hi, lo = split(pad[...].T * (0.5 / STEPS))
        for base in (0, kdim):
            wb[base + k * lanes:base + (k + 1) * lanes, :lanes] = hi
            wb[base + k * lanes:base + (k + 1) * lanes, lanes:] = lo
    padw[...] = zeros(lanes, slots)
    padw[0:nodes, :] = weight_in[...]
    hi, lo = split(padw[...])
    ws[0:lanes] = hi
    ws[lanes:2 * lanes] = hi
    ws[2 * lanes:] = lo
    rows = lax.broadcasted_iota(jnp.int32, (count + 2 * HALO, lanes), 0) + (me * count - HALO)
    state[moved] = jnp.where((rows >= 0) & (rows < count * peers), 1.0, 0.0)

    up = lax.broadcasted_iota(jnp.int32, (slots, slots), 0)
    across = lax.broadcasted_iota(jnp.int32, (slots, slots), 1)
    tri = ones_where(up <= across)
    blocks = order[...]
    source, slot = lax.div(blocks, slots), lax.rem(blocks, slots)
    mine = source == me
    rank = dot(ones_where(mine), tri) - 1.0
    rank = jnp.where(mine, rank, -1.0)
    tall = lax.broadcasted_iota(jnp.int32, (slots, peers), 0)
    wide = lax.broadcasted_iota(jnp.int32, (slots, peers), 1)
    repeat = ones_where(lax.div(tall, pair) == wide)
    rank_all = dot(repeat, rank.astype(jnp.bfloat16))
    slot_all = dot(repeat, slot.astype(jnp.float32).astype(jnp.bfloat16))
    hit = rank_all == lax.rem(up, pair).astype(jnp.float32)
    send_slot = jnp.sum(jnp.where(hit, slot_all, 0.0), axis=1, keepdims=True)
    sends = jnp.where(send_slot == across.astype(jnp.float32), 1.0, 0.0)
    to_send[...] = sends.astype(jnp.bfloat16)
    from_send[...] = sends.T.astype(jnp.bfloat16)
    own = order[pl.ds(me, 1), :]
    own_source = lax.div(own, slots)
    peer_ids = lax.broadcasted_iota(jnp.int32, (peers, slots), 0)
    from_peer = peer_ids == own_source
    seen = dot(ones_where(from_peer), tri) - 1.0
    own_rank = jnp.sum(jnp.where(from_peer, seen, 0.0), axis=0, keepdims=True)
    place = own_source.astype(jnp.float32) * float(pair) + own_rank
    places = jnp.where(up.astype(jnp.float32) == place, 1.0, 0.0)
    to_place[...] = places.astype(jnp.bfloat16)
    from_place[...] = places.T.astype(jnp.bfloat16)
    here = lax.broadcasted_iota(jnp.int32, (1, peers), 1) == me
    limit = jnp.sum(jnp.where(here, counts[...].astype(jnp.float32), 0.0), axis=1, keepdims=True)
    live[...] = jnp.where(lax.broadcasted_iota(jnp.int32, (1, slots), 1).astype(jnp.float32) < limit, 1.0, 0.0)
    for copy in copies:
        copy.wait()


def end_kernel(peers, traces, observed, to_send, from_send, to_place, from_place,
               residual, misfit, adjoint, sent, got, send_sem, recv_sem):
    width, slots = observed.shape
    lanes = sent.shape[-1]
    wide = traces.shape[0]
    pair = slots // peers
    me = lax.axis_index("mx")
    barrier = greet(peers, me)
    synth = traces[...].T
    packed = permute(to_send[...], synth)
    obs = permute(to_place[...], observed[...].T)
    row = jnp.concatenate([packed, obs, zeros(slots, lanes - wide - width)], axis=1)
    sent[...] = row.reshape(peers, pair, lanes)
    pl.semaphore_wait(barrier, peers - 1)

    def copy_to(off):
        dest = lax.rem(me + off, peers)
        return pltpu.make_async_remote_copy(
            src_ref=sent.at[dest], dst_ref=got.at[me], send_sem=send_sem.at[dest], recv_sem=recv_sem.at[me],
            device_id={"mx": dest}, device_id_type=pl.DeviceIdType.MESH)

    def copy_from(off):
        src = lax.rem(me - off + peers, peers)
        return pltpu.make_async_remote_copy(
            src_ref=sent.at[src], dst_ref=got.at[src], send_sem=send_sem.at[src], recv_sem=recv_sem.at[src],
            device_id={"mx": src}, device_id_type=pl.DeviceIdType.MESH)

    def begin(off, _):
        copy_to(off).start()
        return 0

    def finish(off, _):
        copy_from(off).wait_recv()
        return 0

    def drain(off, _):
        copy_to(off).wait_send()
        return 0

    lax.fori_loop(1, peers, begin, 0)
    got[pl.ds(me, 1)] = sent[pl.ds(me, 1)]
    lax.fori_loop(1, peers, finish, 0)
    arrived = got[...].reshape(slots, lanes)
    placed = permute(from_place[...], arrived[:, :wide]).T
    res = placed[width:width + 1] * (placed[:width] - observed[...])
    residual[...] = res
    misfit[...] = 0.5 * jnp.sum(res * res, axis=0, keepdims=True)
    slot_obs = permute(from_send[...], arrived[:, wide:wide + width]).T
    plain = traces[width:width + 1, :] * (traces[0:width, :] - slot_obs)
    a = lax.broadcasted_iota(jnp.int32, (width, width), 0)
    b = lax.broadcasted_iota(jnp.int32, (width, width), 1)
    back = ones_where((lax.div(a, STEPS) == lax.div(b, STEPS)) & (lax.rem(a, STEPS) + lax.rem(b, STEPS) == STEPS - 1))
    adjoint[...] = permute(back, plain)
    lax.fori_loop(1, peers, drain, 0)


def wave_kernel(state, wb, ws, elem, live, cpl, out, ubuf, lhs, hist):
    fields = ubuf.shape[1]
    lanes = state.shape[2]
    count = state.shape[1] - 2 * HALO
    first = GUARD + HALO
    kdim = wb.shape[0] // 2
    rows_all = ubuf.shape[2]
    metric = state.at[fields:fields + 3]
    mask = state.at[fields + 3]
    for b in range(2):
        for f in range(fields):
            ubuf[b, f, 0:GUARD] = zeros(GUARD, lanes)
            ubuf[b, f, rows_all - GUARD:] = zeros(GUARD, lanes)
            if b:
                ubuf[b, f] = zeros(rows_all, lanes)
            else:
                ubuf[b, f, GUARD:rows_all - GUARD] = state[f] * mask[...]

    def mix(src, c, halo, slab):
        rows = count + 2 * halo
        base = first - halo
        for gi in range(3):
            g = c * 3 + gi
            for r in range(0, rows, slab):
                acc = [None] * 3
                for f in range(fields):
                    uf = ubuf[src, f, base + r:base + r + slab]
                    for k in range(3):
                        term = cpl[(k * fields + g) * fields + f] * uf
                        acc[k] = term if acc[k] is None else acc[k] + term
                at = gi * rows + r
                mid = ubuf[src, g, base + r:base + r + slab]
                vals = [acc[k] * metric[k, HALO - halo + r:HALO - halo + r + slab] for k in range(3)]
                vals.append(ubuf[src, g, base + r - 1:base + r - 1 + slab] - mid)
                vals.append(ubuf[src, g, base + r + 1:base + r + 1 + slab] - mid)
                for k, v in enumerate(vals):
                    hi, lo = split(v)
                    lhs[c, at:at + slab, k * lanes:(k + 1) * lanes] = hi
                    lhs[c, at:at + slab, kdim + k * lanes:kdim + (k + 1) * lanes] = lo

    def apply(src, dst, c, halo):
        rows = count + 2 * halo
        base = first - halo
        res = jnp.dot(lhs[c, :3 * rows], wb[...], preferred_element_type=jnp.float32)
        for gi in range(3):
            g = c * 3 + gi
            part = res[gi * rows:(gi + 1) * rows]
            new = ubuf[src, g, base:base + rows] + (part[:, :lanes] + part[:, lanes:])
            ubuf[dst, g, base:base + rows] = new * mask[HALO - halo:HALO - halo + rows]

    def step(halo, slab, t, _):
        src = lax.rem(t, 2)
        dst = 1 - src
        mix(src, 0, halo, slab)
        mix(src, 1, halo, slab)
        apply(src, dst, 0, halo)
        mix(src, 2, halo, slab)
        apply(src, dst, 1, halo)
        apply(src, dst, 2, halo)
        mine = slice(first, first + count)
        vals = [ubuf[dst, c, mine] for c in range(3)]
        vals.append((ubuf[dst, 3, mine] + ubuf[dst, 4, mine] + ubuf[dst, 5, mine]) / 3.0)
        for c, v in enumerate(vals):
            hi, lo = split(v)
            hist[t, c, :, 0:lanes] = hi
            hist[t, c, :, lanes:2 * lanes] = lo
            hist[t, c, :, 2 * lanes:] = hi
        return 0

    lax.fori_loop(0, 3, functools.partial(step, 16, 80), 0)
    lax.fori_loop(3, STEPS, functools.partial(step, 8, 48), 0)

    slots = ws.shape[1]
    ids = lax.broadcasted_iota(jnp.int32, (count, slots), 0)
    pick = jnp.where(ids == elem[...], live[...], 0.0)

    out[...] = zeros(*out.shape)
    out[COMPS * STEPS:COMPS * STEPS + 1, :] = live[...]

    def sample(t, _):
        for c in range(COMPS):
            prod = jnp.dot(hist[t, c], ws[...], preferred_element_type=jnp.float32)
            out[pl.ds(c * STEPS + t, 1), :] = jnp.sum(prod * pick, axis=0, keepdims=True)
        return 0

    lax.fori_loop(0, STEPS, sample, 0)


VM = pl.BlockSpec(memory_space=pltpu.VMEM)


def shards(initial, derivative, coupling, face_lift, metric, rec_element, rec_weight, live_counts, shot_order, observed):
    fields, nodes, count = initial.shape
    lanes = -(-nodes // 128) * 128
    slots, width = observed.shape
    peers = lax.axis_size("mx")
    span = count + 2 * HALO
    kdim = (derivative.shape[0] + face_lift.shape[0]) * lanes
    wide = -(-(width + 1) // 64) * 64
    f32, bf16 = jnp.float32, jnp.bfloat16
    square = jax.ShapeDtypeStruct((slots, slots), bf16)
    state, wb, ws, to_send, from_send, to_place, from_place, live = pl.pallas_call(
        functools.partial(start_kernel, peers),
        out_shape=(
            jax.ShapeDtypeStruct((fields + metric.shape[0] + 1, span, lanes), f32),
            jax.ShapeDtypeStruct((2 * kdim, 2 * lanes), bf16),
            jax.ShapeDtypeStruct((3 * lanes, slots), bf16),
            square, square, square, square,
            jax.ShapeDtypeStruct((1, slots), f32),
        ),
        in_specs=[VM] * 7,
        out_specs=[VM] * 8,
        scratch_shapes=[
            pltpu.VMEM((lanes, lanes), f32),
            pltpu.VMEM((lanes, slots), f32),
            pltpu.SemaphoreType.DMA((2,)),
            pltpu.SemaphoreType.DMA((2,)),
        ],
        compiler_params=pltpu.CompilerParams(collective_id=0, has_side_effects=True),
        name="start",
    )(initial, metric, derivative, face_lift, rec_weight, shot_order.reshape(peers, slots), live_counts[None, :])
    traces = pl.pallas_call(
        wave_kernel,
        out_shape=jax.ShapeDtypeStruct((wide, slots), f32),
        in_specs=[VM] * 5 + [pl.BlockSpec(memory_space=pltpu.SMEM)],
        out_specs=VM,
        scratch_shapes=[
            pltpu.VMEM((2, fields, span + 2 * GUARD, lanes), f32),
            pltpu.VMEM((3, 3 * span, 2 * kdim), bf16),
            pltpu.VMEM((STEPS, COMPS, count, 3 * lanes), bf16),
        ],
        name="waves",
    )(state, wb, ws, rec_element[None, :], live, coupling.reshape(-1))
    residual, misfit, adjoint = pl.pallas_call(
        functools.partial(end_kernel, peers),
        out_shape=(
            jax.ShapeDtypeStruct((width, slots), f32),
            jax.ShapeDtypeStruct((1, slots), f32),
            jax.ShapeDtypeStruct((width, slots), f32),
        ),
        in_specs=[VM] * 6,
        out_specs=[VM] * 3,
        scratch_shapes=[
            pltpu.VMEM((peers, slots // peers, lanes), f32),
            pltpu.VMEM((peers, slots // peers, lanes), f32),
            pltpu.SemaphoreType.DMA((peers,)),
            pltpu.SemaphoreType.DMA((peers,)),
        ],
        compiler_params=pltpu.CompilerParams(collective_id=1, has_side_effects=True),
        name="finish",
    )(traces, observed.T, to_send, from_send, to_place, from_place)
    return residual.T, misfit[0], adjoint.T


def solution(mesh):
    in_specs = (
        P("shots", None, "mx"),
        P(),
        P(),
        P(),
        P(None, "mx"),
        P("mx"),
        P(None, "mx"),
        P(),
        P(),
        P(("shots", "mx"), None),
    )
    out_specs = (P(("shots", "mx"), None), P(("shots", "mx")), P(("shots", "mx"), None))
    return jax.shard_map(shards, mesh=mesh, in_specs=in_specs, out_specs=out_specs, check_vma=False)
```

profile of v0, /device:TPU:0, one launch (start us, length us, event | category | flops | bytes accessed | tf_op | source)
XLA Modules:
  0.0 67.6 jit_solution(16065262305417792579)
XLA Ops:
  0.6 0.0 copy-start
  0.6 1.6 %copy.14.face_lift = f32[2,125,125]{2,1,0:T(8,128)} copy(f32[2,125,125]{2,0,1:T(2,128)} %param.13) | data formatting | bytes 250000 | tf_op args[3]
  2.2 1.3 %reshape.12.order = s32[16,256]{1,0:T(8,128)} reshape(s32[4096]{0:T(1024)} %param.18) | data formatting | bytes 32768 | tf_op jit(solution)/shard_map/reshape | solution.py:308
  3.5 11.2 %start.1 = (f32[13,160,128]{2,1,0:T(8,128)}, bf16[1280,256]{1,0:T(8,128)(2,1)}, bf16[384,256]{1,0:T(8,128)(2,1)}, bf16[256,256]{1,0:T(8,128)(2,1)}, bf16[256,256...) custom-call(f32[9,125,128]{2,1,0:T(8,128)} %initial.1, ...), custom_call_target="tpu_custom_call" | custom-call | tf_op jit(solution)/shard_map/start/pallas_call | solution.py:289
  14.7 0.0 copy-done
  14.8 0.7 reshape.13.cpl
  15.4 38.2 %waves.1.traces = f32[64,256]{1,0:T(8,128)} custom-call(f32[13,160,128]{2,1,0:T(8,128)} %get-tuple-element.14.state, bf16[1280,256]{1,0:T(8,128)(2,1)} %get-tuple-element.15.wb, bf16[384,256]{1,0:T(8,128)(2,1)} %get-tuple-element.16.ws, s32[1,256]{1,0:T(1,128)} %bitcast.9, f32[1,256]{1,0:T(1,128)} %get-tuple-element.17.live, f32[243]{0:T(256)} %reshape.13.cpl), custom_call_target="tpu_custom_call" | custom-call | tf_op jit(solution)/shard_map/waves/pallas_call | solution.py:309
  53.7 9.8 %finish.1 = (f32[48,256]{1,0:T(8,128)}, f32[1,256]{1,0:T(1,128)}, f32[48,256]{1,0:T(8,128)}) custom-call(f32[64,256]{1,0:T(8,128)} %waves.1.traces, f32[48,256]{1,0:T(8,128)} %bitcast.6, bf16[256,256]{1,0:T(8,128)(2,1)} %get-tuple-element.18.to_send, bf16[256,256]{1,0:T(8,128)(2,1)} %get-tuple-element.19.from_send, ...), custom_call_target="tpu_custom_call" | custom-call | tf_op jit(solution)/shard_map/finish/pallas_call | solution.py:321
  63.5 1.4 %copy.19 = f32[256,48]{0,1:T(8,128)} copy(f32[256,48]{0,1:T(8,128)} %bitcast.8) | data formatting | bytes 98304
  64.9 1.2 %copy.20 = f32[256]{0:T(256)} copy(f32[256]{0:T(256)} %bitcast.10) | data formatting | bytes 2048
  66.2 1.4 %copy.21 = f32[256,48]{0,1:T(8,128)} copy(f32[256,48]{0,1:T(8,128)} %bitcast.7) | data formatting | bytes 98304
  (1 shorter events, 0.0 us)
Async XLA Ops:
  0.6 14.1 %copy-start = (f32[3,9,9]{2,0,1:T(4,128)S(1)}, f32[3,9,9]{2,0,1:T(4,128)}, u32[]{:S(2)}) copy-start(f32[3,9,9]{2,0,1:T(4,128)} %param.12) | copy-start | bytes 2920
where the time goes:
time: 68 us; the launch traced here: 67.6 us
  Pallas kernels  59.3 us (87%)
  local copies, waits for them, and re-layouts  7.64 us (11%)
    pallas_call x1, Pallas kernels, shards(): pl.pallas_call(wave_kernel, out_shape=jax.ShapeDtypeStruct((wide, slots),...  38.2 us
    pallas_call x1, Pallas kernels, shards(): pl.pallas_call(functools.partial(start_kernel, peers), out_shape=(jax.Sha...  11.2 us
    pallas_call x1, Pallas kernels, shards(): pl.pallas_call(functools.partial(end_kernel, peers), out_shape=(jax.Shape...  9.84 us
    unnamed x7, local copies, waits for them, and re-layouts  5.65 us

commit v1 on v0

--- a/solution.py
+++ b/solution.py
@@ -10,6 +10,10 @@
 COMPS = 4
 HALO = 16
 GUARD = 8
+TILE = 16
+SUB = 8
+AHEAD = 3
+WIDE = 4
 
 
 def split(x):
@@ -78,13 +82,20 @@
         copies[-1].start()
     pad[...] = zeros(lanes, lanes)
     turns = derivative.shape[0]
-    kdim = (turns + face_lift.shape[0]) * lanes
-    for k in range(kdim // lanes):
-        pad[0:nodes, 0:nodes] = derivative[k] if k < turns else face_lift[k - turns]
+
+    def weigh(k, matrix):
+        pad[0:nodes, 0:nodes] = matrix
         hi, lo = split(pad[...].T * (0.5 / STEPS))
-        for base in (0, kdim):
-            wb[base + k * lanes:base + (k + 1) * lanes, :lanes] = hi
-            wb[base + k * lanes:base + (k + 1) * lanes, lanes:] = lo
+        at = slice(k * lanes, (k + 1) * lanes)
+        wb[0:lanes, at] = hi
+        wb[lanes:2 * lanes, at] = hi
+        wb[2 * lanes:, at] = lo
+
+    for k in range(turns):
+        weigh(k, derivative[k])
+    weigh(turns, face_lift[0])
+    weigh(turns + 1, face_lift[1])
+    weigh(turns + 2, -(face_lift[0] + face_lift[1]))
     padw[...] = zeros(lanes, slots)
     padw[0:nodes, :] = weight_in[...]
     hi, lo = split(padw[...])
@@ -185,92 +196,126 @@
     lax.fori_loop(1, peers, drain, 0)
 
 
-def wave_kernel(state, wb, ws, elem, live, cpl, out, ubuf, lhs, hist):
-    fields = ubuf.shape[1]
-    lanes = state.shape[2]
-    count = state.shape[1] - 2 * HALO
-    first = GUARD + HALO
-    kdim = wb.shape[0] // 2
-    rows_all = ubuf.shape[2]
-    metric = state.at[fields:fields + 3]
-    mask = state.at[fields + 3]
-    for b in range(2):
+def wave_kernel(state, wb, ws, elem, live, cpl, out, u, x, xp, turned, faces, pick, rows_out, mixer):
+    fields, total, lanes = u.shape
+    span = state.shape[1]
+    count = span - 2 * HALO
+    kinds = turned.shape[0] - 1
+    margin = (total - span) // 2
+    own = margin + HALO
+    slots = ws.shape[1]
+    groups = total // TILE
+
+    def stored(f, r, n):
+        return state[f, r - margin:r - margin + n]
+
+    def put(grp, f, new):
+        hi, lo = split(new)
+        x[grp, f * TILE:(f + 1) * TILE, 0:lanes] = hi
+        x[grp, f * TILE:(f + 1) * TILE, lanes:] = lo
+
+    for f in range(fields):
+        u[f, 0:margin] = zeros(margin, lanes)
+        u[f, total - margin:] = zeros(margin, lanes)
+        u[f, margin:total - margin] = state[f] * state[fields + kinds]
+        for k in range(2):
+            faces[k, f, 0:GUARD] = zeros(GUARD, lanes)
+            faces[k, f, GUARD + total:] = zeros(GUARD, lanes)
+        for grp in range(groups):
+            put(grp, f, u[f, grp * TILE:(grp + 1) * TILE])
+
+    for i in range(mixer.shape[0]):
+        mixer[i] = jnp.full((SUB, lanes), cpl[i], jnp.float32)
+    first, last = own // TILE, (own + count - 1) // TILE
+    ids = lax.broadcasted_iota(jnp.int32, pick.shape, 0) + (first * TILE - own)
+    pick[...] = jnp.where(ids == elem[...], live[...], 0.0)
+    xp[...] = jnp.zeros(xp.shape, xp.dtype)
+
+    def spread(grp):
+        lhs = x[grp]
+        res = dot(lhs, wb[0:2 * lanes]) + dot(lhs[:, 0:lanes], wb[2 * lanes:])
+        at = slice(grp * TILE, (grp + 1) * TILE)
+        shifted = slice(GUARD + grp * TILE, GUARD + (grp + 1) * TILE)
         for f in range(fields):
-            ubuf[b, f, 0:GUARD] = zeros(GUARD, lanes)
-            ubuf[b, f, rows_all - GUARD:] = zeros(GUARD, lanes)
-            if b:
-                ubuf[b, f] = zeros(rows_all, lanes)
+            part = res[f * TILE:(f + 1) * TILE]
+            for k in range(kinds):
+                turned[k, f, at] = part[:, k * lanes:(k + 1) * lanes]
+            for k in range(2):
+                faces[k, f, shifted] = part[:, (kinds + k) * lanes:(kinds + k + 1) * lanes]
+            turned[kinds, f, at] = part[:, (kinds + 2) * lanes:]
+
+    def advance(grp):
+        top, rows = grp * TILE, TILE
+        if grp == 0:
+            top, rows = top + margin, rows - margin
+        if grp == groups - 1:
+            rows = rows - margin
+        at = slice(top, top + rows)
+        parts = [slice(top + r, top + r + SUB) for r in range(0, rows, SUB)]
+        acc = [[None] * fields for _ in parts]
+        for k in range(kinds):
+            m = [stored(fields + k, top + p * SUB, SUB) for p in range(len(parts))]
+            for row in range(fields):
+                part_sum = [None] * len(parts)
+                for f in range(fields):
+                    weight = mixer[(k * fields + row) * fields + f]
+                    for p, part in enumerate(parts):
+                        term = weight * turned[k, f, part]
+                        part_sum[p] = term if f == 0 else part_sum[p] + term
+                for p in range(len(parts)):
+                    term = part_sum[p] * m[p]
+                    acc[p][row] = term if k == 0 else acc[p][row] + term
+        acc = [jnp.concatenate(list(rows_of), axis=0) for rows_of in zip(*acc)]
+        fresh = []
+        for f in range(fields):
+            side = faces[0, f, GUARD + top - 1:GUARD + top - 1 + rows] + faces[1, f, GUARD + top + 1:GUARD + top + 1 + rows]
+            new = u[f, at] + ((acc[f] + turned[kinds, f, at]) + side)
+            if top < own or top + rows > own + count:
+                new = new * stored(fields + kinds, top, rows)
+            u[f, at] = new
+            fresh.append(new)
+        if first <= grp <= last:
+            hi, lo = split((fresh[3] + fresh[4] + fresh[5]) * (1.0 / 3.0))
+            xp[(grp - first) * TILE:(grp - first + 1) * TILE, 0:lanes] = hi
+            xp[(grp - first) * TILE:(grp - first + 1) * TILE, lanes:] = lo
+        for f in range(fields):
+            new = fresh[f]
+            if grp == 0:
+                new = jnp.concatenate([zeros(margin, lanes), new], axis=0)
+            if grp == groups - 1:
+                new = jnp.concatenate([new, zeros(margin, lanes)], axis=0)
+            put(grp, f, new)
+
+    def sample(t):
+        for c in range(COMPS):
+            if c < 3:
+                lhs = x[first:last + 1, c * TILE:(c + 1) * TILE].reshape(pick.shape[0], 2 * lanes)
             else:
-                ubuf[b, f, GUARD:rows_all - GUARD] = state[f] * mask[...]
-
-    def mix(src, c, halo, slab):
-        rows = count + 2 * halo
-        base = first - halo
-        for gi in range(3):
-            g = c * 3 + gi
-            for r in range(0, rows, slab):
-                acc = [None] * 3
-                for f in range(fields):
-                    uf = ubuf[src, f, base + r:base + r + slab]
-                    for k in range(3):
-                        term = cpl[(k * fields + g) * fields + f] * uf
-                        acc[k] = term if acc[k] is None else acc[k] + term
-                at = gi * rows + r
-                mid = ubuf[src, g, base + r:base + r + slab]
-                vals = [acc[k] * metric[k, HALO - halo + r:HALO - halo + r + slab] for k in range(3)]
-                vals.append(ubuf[src, g, base + r - 1:base + r - 1 + slab] - mid)
-                vals.append(ubuf[src, g, base + r + 1:base + r + 1 + slab] - mid)
-                for k, v in enumerate(vals):
-                    hi, lo = split(v)
-                    lhs[c, at:at + slab, k * lanes:(k + 1) * lanes] = hi
-                    lhs[c, at:at + slab, kdim + k * lanes:kdim + (k + 1) * lanes] = lo
-
-    def apply(src, dst, c, halo):
-        rows = count + 2 * halo
-        base = first - halo
-        res = jnp.dot(lhs[c, :3 * rows], wb[...], preferred_element_type=jnp.float32)
-        for gi in range(3):
-            g = c * 3 + gi
-            part = res[gi * rows:(gi + 1) * rows]
-            new = ubuf[src, g, base:base + rows] + (part[:, :lanes] + part[:, lanes:])
-            ubuf[dst, g, base:base + rows] = new * mask[HALO - halo:HALO - halo + rows]
-
-    def step(halo, slab, t, _):
-        src = lax.rem(t, 2)
-        dst = 1 - src
-        mix(src, 0, halo, slab)
-        mix(src, 1, halo, slab)
-        apply(src, dst, 0, halo)
-        mix(src, 2, halo, slab)
-        apply(src, dst, 1, halo)
-        apply(src, dst, 2, halo)
-        mine = slice(first, first + count)
-        vals = [ubuf[dst, c, mine] for c in range(3)]
-        vals.append((ubuf[dst, 3, mine] + ubuf[dst, 4, mine] + ubuf[dst, 5, mine]) / 3.0)
-        for c, v in enumerate(vals):
-            hi, lo = split(v)
-            hist[t, c, :, 0:lanes] = hi
-            hist[t, c, :, lanes:2 * lanes] = lo
-            hist[t, c, :, 2 * lanes:] = hi
+                lhs = xp[...]
+            prod = dot(lhs, ws[0:2 * lanes]) + dot(lhs[:, 0:lanes], ws[2 * lanes:])
+            rows_out[t, c:c + 1, :] = jnp.sum(prod * pick[...], axis=0, keepdims=True)
+
+    def step(todo, ahead, t, _):
+        sample(t)
+        for j, grp in enumerate(todo):
+            spread(todo[(j + ahead) % len(todo)])
+            advance(grp)
         return 0
 
-    lax.fori_loop(0, 3, functools.partial(step, 16, 80), 0)
-    lax.fori_loop(3, STEPS, functools.partial(step, 8, 48), 0)
-
-    slots = ws.shape[1]
-    ids = lax.broadcasted_iota(jnp.int32, (count, slots), 0)
-    pick = jnp.where(ids == elem[...], live[...], 0.0)
-
+    for grp in range(AHEAD):
+        spread(grp)
+    lax.fori_loop(0, WIDE, functools.partial(step, tuple(range(groups)), AHEAD), 0)
+    lax.fori_loop(WIDE, STEPS, functools.partial(step, tuple(range(first, last + 1)), AHEAD - 1), 0)
+    sample(STEPS)
     out[...] = zeros(*out.shape)
+    for c in range(COMPS):
+        for t in range(STEPS):
+            out[c * STEPS + t:c * STEPS + t + 1, :] = rows_out[t + 1, c:c + 1, :]
     out[COMPS * STEPS:COMPS * STEPS + 1, :] = live[...]
 
-    def sample(t, _):
-        for c in range(COMPS):
-            prod = jnp.dot(hist[t, c], ws[...], preferred_element_type=jnp.float32)
-            out[pl.ds(c * STEPS + t, 1), :] = jnp.sum(prod * pick, axis=0, keepdims=True)
-        return 0
-
-    lax.fori_loop(0, STEPS, sample, 0)
+
+def vm(x):
+    return pltpu.with_memory_space_constraint(x, pltpu.VMEM)
 
 
 VM = pl.BlockSpec(memory_space=pltpu.VMEM)
@@ -282,18 +327,20 @@
     slots, width = observed.shape
     peers = lax.axis_size("mx")
     span = count + 2 * HALO
-    kdim = (derivative.shape[0] + face_lift.shape[0]) * lanes
+    kinds = derivative.shape[0]
+    total = span + TILE
+    picked = count + TILE
     wide = -(-(width + 1) // 64) * 64
     f32, bf16 = jnp.float32, jnp.bfloat16
-    square = jax.ShapeDtypeStruct((slots, slots), bf16)
+    square = pltpu.VMEM((slots, slots), bf16)
     state, wb, ws, to_send, from_send, to_place, from_place, live = pl.pallas_call(
         functools.partial(start_kernel, peers),
         out_shape=(
-            jax.ShapeDtypeStruct((fields + metric.shape[0] + 1, span, lanes), f32),
-            jax.ShapeDtypeStruct((2 * kdim, 2 * lanes), bf16),
-            jax.ShapeDtypeStruct((3 * lanes, slots), bf16),
+            pltpu.VMEM((fields + metric.shape[0] + 1, span, lanes), f32),
+            pltpu.VMEM((3 * lanes, (kinds + 3) * lanes), bf16),
+            pltpu.VMEM((3 * lanes, slots), bf16),
             square, square, square, square,
-            jax.ShapeDtypeStruct((1, slots), f32),
+            pltpu.VMEM((1, slots), f32),
         ),
         in_specs=[VM] * 7,
         out_specs=[VM] * 8,
@@ -308,22 +355,27 @@
     )(initial, metric, derivative, face_lift, rec_weight, shot_order.reshape(peers, slots), live_counts[None, :])
     traces = pl.pallas_call(
         wave_kernel,
-        out_shape=jax.ShapeDtypeStruct((wide, slots), f32),
+        out_shape=pltpu.VMEM((wide, slots), f32),
         in_specs=[VM] * 5 + [pl.BlockSpec(memory_space=pltpu.SMEM)],
         out_specs=VM,
         scratch_shapes=[
-            pltpu.VMEM((2, fields, span + 2 * GUARD, lanes), f32),
-            pltpu.VMEM((3, 3 * span, 2 * kdim), bf16),
-            pltpu.VMEM((STEPS, COMPS, count, 3 * lanes), bf16),
+            pltpu.VMEM((fields, total, lanes), f32),
+            pltpu.VMEM((total // TILE, fields * TILE, 2 * lanes), bf16),
+            pltpu.VMEM((picked, 2 * lanes), bf16),
+            pltpu.VMEM((kinds + 1, fields, total, lanes), f32),
+            pltpu.VMEM((2, fields, total + 2 * GUARD, lanes), f32),
+            pltpu.VMEM((picked, slots), f32),
+            pltpu.VMEM((STEPS + 1, 8, slots), f32),
+            pltpu.VMEM((coupling.size, SUB, lanes), f32),
         ],
         name="waves",
-    )(state, wb, ws, rec_element[None, :], live, coupling.reshape(-1))
+    )(vm(state), vm(wb), vm(ws), rec_element[None, :], vm(live), coupling.reshape(-1))
     residual, misfit, adjoint = pl.pallas_call(
         functools.partial(end_kernel, peers),
         out_shape=(
-            jax.ShapeDtypeStruct((width, slots), f32),
-            jax.ShapeDtypeStruct((1, slots), f32),
-            jax.ShapeDtypeStruct((width, slots), f32),
+            pltpu.VMEM((width, slots), f32),
+            pltpu.VMEM((1, slots), f32),
+            pltpu.VMEM((width, slots), f32),
         ),
         in_specs=[VM] * 6,
         out_specs=[VM] * 3,
@@ -335,7 +387,7 @@
         ],
         compiler_params=pltpu.CompilerParams(collective_id=1, has_side_effects=True),
         name="finish",
-    )(traces, observed.T, to_send, from_send, to_place, from_place)
+    )(vm(traces), observed.T, vm(to_send), vm(from_send), vm(to_place), vm(from_place))
     return residual.T, misfit[0], adjoint.T
 
 

time: 68 us -> 51.5 us (0.76)
  Pallas kernels: 59.3 us -> 45.2 us
  local copies, waits for them, and re-layouts: 7.64 us -> 5.37 us
    pallas_call x3, Pallas kernels: 59.3 us -> 45.2 us  [the longest x1 26.6 us: shards(): pl.pallas_call(wave_kernel, out_shape=pltpu.VMEM((wide, slots), f32), in_...]
    unnamed x7, local copies, waits for them, and re-layouts: 5.65 us -> 3.38 us
where the time goes in v1:
time: 51.5 us; the launch traced here: 51.3 us
  Pallas kernels  45.2 us (88%)
  local copies, waits for them, and re-layouts  5.37 us (10%)
  between operations  0.67 us (1%)
    pallas_call x1, Pallas kernels, shards(): pl.pallas_call(wave_kernel, out_shape=pltpu.VMEM((wide, slots), f32), in_...  26.6 us
    pallas_call x1, Pallas kernels, shards(): pl.pallas_call(functools.partial(start_kernel, peers), out_shape=(pltpu.V...  9.73 us
    pallas_call x1, Pallas kernels, shards(): pl.pallas_call(functools.partial(end_kernel, peers), out_shape=(pltpu.VME...  8.87 us
    unnamed x7, local copies, waits for them, and re-layouts  3.38 us
    reshape x1, local copies, waits for them, and re-layouts, shards(): shot_order.reshape(peers, slots)  1.33 us

profile of v1, /device:TPU:0, one launch (start us, length us, event | category | flops | bytes accessed | tf_op | source)
XLA Modules:
  0.0 51.3 jit_solution(1942691582526082921)
XLA Ops:
  0.6 0.0 copy-start
  0.6 1.6 %copy.14.face_lift = f32[2,125,125]{2,1,0:T(8,128)} copy(f32[2,125,125]{2,0,1:T(2,128)} %param.13) | data formatting | bytes 250000 | tf_op args[3]
  2.2 1.3 %reshape.12.order = s32[16,256]{1,0:T(8,128)} reshape(s32[4096]{0:T(1024)} %param.18) | data formatting | bytes 32768 | tf_op jit(solution)/shard_map/reshape | solution.py:355
  3.5 9.7 %start.1 = (f32[13,160,128]{2,1,0:T(8,128)S(1)}, bf16[384,768]{1,0:T(8,128)(2,1)S(1)}, bf16[384,256]{1,0:T(8,128)(2,1)S(1)}, bf16[256,256]{1,0:T(8,128)(2,1)S(1)...) custom-call(f32[9,125,128]{2,1,0:T(8,128)} %initial.1, ...), custom_call_target="tpu_custom_call" | custom-call | tf_op jit(solution)/shard_map/start/pallas_call | solution.py:336
  13.3 0.0 copy-done
  13.3 0.7 %reshape.13.cpl = f32[243]{0:T(256)} reshape(f32[3,9,9]{2,1,0:T(8,128)S(1)} %copy.15) | data formatting | bytes 1944 | tf_op jit(solution)/shard_map/reshape | solution.py:372
  14.0 26.6 %waves.1.traces = f32[64,256]{1,0:T(8,128)S(1)} custom-call(f32[13,160,128]{2,1,0:T(8,128)S(1)} %get-tuple-element.14.state, bf16[384,768]{1,0:T(8,128)(2,1)S(1)} %get-tuple-element.15.wb, bf16[384,256]{1,0:T(8,128)(2,1)S(1)} %get-tuple-element.16.ws, s32[1,256]{1,0:T(1,128)} %bitcast.10, f32[1,256]{1,0:T(1,128)S(1)} %get-tuple-element.17.live, f32[243]{0:T(256)} %reshape.13.cpl), custom_call_target="tpu_custom_call" | custom-call | tf_op jit(solution)/shard_map/waves/pallas_call | solution.py:356
  40.6 8.9 %finish.1 = (f32[48,256]{1,0:T(8,128)S(1)}, f32[1,256]{1,0:T(1,128)S(1)}, f32[48,256]{1,0:T(8,128)S(1)}) custom-call(f32[64,256]{1,0:T(8,128)S(1)} %waves.1.traces, f32[48,256]{1,0:T(8,128)} %bitcast.9, bf16[256,256]{1,0:T(8,128)(2,1)S(1)} %get-tuple-element.18.to_send, bf16[256,256]{1,0:T(8,128)(2,1)S(1)} %get-tuple-element.19.from_send, ...), custom_call_target="tpu_custom_call" | custom-call | tf_op jit(solution)/shard_map/finish/pallas_call | solution.py:373
  49.5 0.6 %copy.19 = f32[256,48]{0,1:T(8,128)} copy(f32[256,48]{0,1:T(8,128)S(1)} %bitcast.7) | data formatting | bytes 98304
  50.1 0.6 %copy.21 = f32[256,48]{0,1:T(8,128)} copy(f32[256,48]{0,1:T(8,128)S(1)} %bitcast.6) | data formatting | bytes 98304
  50.7 0.6 %copy.20 = f32[256]{0:T(256)} copy(f32[256]{0:T(256)S(1)} %bitcast.8) | data formatting | bytes 2048
  (1 shorter events, 0.0 us)
Async XLA Ops:
  0.6 12.6 %copy-start = (f32[3,9,9]{2,0,1:T(4,128)S(1)}, f32[3,9,9]{2,0,1:T(4,128)}, u32[]{:S(2)}) copy-start(f32[3,9,9]{2,0,1:T(4,128)} %param.12) | copy-start | bytes 2920

commit v2 on v1

--- a/solution.py
+++ b/solution.py
@@ -14,6 +14,7 @@
 SUB = 8
 AHEAD = 3
 WIDE = 4
+GRANT = 32 * 2 ** 20
 
 
 def split(x):
@@ -52,12 +53,13 @@
     return barrier
 
 
-def start_kernel(peers, initial, metric, derivative, face_lift, weight_in, order, counts,
-                 state, wb, ws, to_send, from_send, to_place, from_place, live,
+def start_kernel(peers, initial, metric, derivative, face_lift, weight_in, order, counts, elem, coupling,
+                 state, wb, ws, to_send, from_send, to_place, from_place, live, mixer, pick,
                  pad, padw, send_sem, recv_sem):
     fields, nodes, count = initial.shape
     lanes = pad.shape[0]
-    slots = order.shape[1]
+    slots = padw.shape[1]
+    pieces = slots // lanes
     pair = slots // peers
     me = lax.axis_index("mx")
     right, left = lax.rem(me + 1, peers), lax.rem(me + peers - 1, peers)
@@ -93,9 +95,10 @@
 
     for k in range(turns):
         weigh(k, derivative[k])
-    weigh(turns, face_lift[0])
-    weigh(turns + 1, face_lift[1])
-    weigh(turns + 2, -(face_lift[0] + face_lift[1]))
+    lower, upper = face_lift[:, 0, :], face_lift[:, 1, :]
+    weigh(turns, lower)
+    weigh(turns + 1, upper)
+    weigh(turns + 2, -(lower + upper))
     padw[...] = zeros(lanes, slots)
     padw[0:nodes, :] = weight_in[...]
     hi, lo = split(padw[...])
@@ -108,7 +111,7 @@
     up = lax.broadcasted_iota(jnp.int32, (slots, slots), 0)
     across = lax.broadcasted_iota(jnp.int32, (slots, slots), 1)
     tri = ones_where(up <= across)
-    blocks = order[...]
+    blocks = jnp.concatenate([order[pl.ds(i, peers, stride=pieces), :] for i in range(pieces)], axis=1)
     source, slot = lax.div(blocks, slots), lax.rem(blocks, slots)
     mine = source == me
     rank = dot(ones_where(mine), tri) - 1.0
@@ -123,7 +126,7 @@
     sends = jnp.where(send_slot == across.astype(jnp.float32), 1.0, 0.0)
     to_send[...] = sends.astype(jnp.bfloat16)
     from_send[...] = sends.T.astype(jnp.bfloat16)
-    own = order[pl.ds(me, 1), :]
+    own = jnp.concatenate([order[pl.ds(me * pieces + i, 1), :] for i in range(pieces)], axis=1)
     own_source = lax.div(own, slots)
     peer_ids = lax.broadcasted_iota(jnp.int32, (peers, slots), 0)
     from_peer = peer_ids == own_source
@@ -135,7 +138,15 @@
     from_place[...] = places.T.astype(jnp.bfloat16)
     here = lax.broadcasted_iota(jnp.int32, (1, peers), 1) == me
     limit = jnp.sum(jnp.where(here, counts[...].astype(jnp.float32), 0.0), axis=1, keepdims=True)
-    live[...] = jnp.where(lax.broadcasted_iota(jnp.int32, (1, slots), 1).astype(jnp.float32) < limit, 1.0, 0.0)
+    alive = jnp.where(lax.broadcasted_iota(jnp.int32, (1, slots), 1).astype(jnp.float32) < limit, 1.0, 0.0)
+    live[...] = alive
+    ids = lax.broadcasted_iota(jnp.int32, pick.shape, 0) - (pick.shape[0] - count) // 2
+    pick[...] = jnp.where(ids == elem[...], alive, 0.0)
+    for row in range(fields):
+        for k in range(kinds):
+            line = coupling[row, k:k + 1, :]
+            for f in range(fields):
+                mixer[(k * fields + row) * fields + f] = jnp.broadcast_to(line[:, f:f + 1], (SUB, lanes))
     for copy in copies:
         copy.wait()
 
@@ -150,10 +161,15 @@
     barrier = greet(peers, me)
     synth = traces[...].T
     packed = permute(to_send[...], synth)
-    obs = permute(to_place[...], observed[...].T)
+    a = lax.broadcasted_iota(jnp.int32, (width, width), 0)
+    b = lax.broadcasted_iota(jnp.int32, (width, width), 1)
+    back = ones_where((lax.div(a, STEPS) == lax.div(b, STEPS)) & (lax.rem(a, STEPS) + lax.rem(b, STEPS) == STEPS - 1))
+    obs = permute(to_place[...], permute(back, observed[...]).T)
     row = jnp.concatenate([packed, obs, zeros(slots, lanes - wide - width)], axis=1)
     sent[...] = row.reshape(peers, pair, lanes)
     pl.semaphore_wait(barrier, peers - 1)
+
+    turned = traces[width:width + 1, :] * permute(back, traces[0:width, :])
 
     def copy_to(off):
         dest = lax.rem(me + off, peers)
@@ -188,15 +204,11 @@
     residual[...] = res
     misfit[...] = 0.5 * jnp.sum(res * res, axis=0, keepdims=True)
     slot_obs = permute(from_send[...], arrived[:, wide:wide + width]).T
-    plain = traces[width:width + 1, :] * (traces[0:width, :] - slot_obs)
-    a = lax.broadcasted_iota(jnp.int32, (width, width), 0)
-    b = lax.broadcasted_iota(jnp.int32, (width, width), 1)
-    back = ones_where((lax.div(a, STEPS) == lax.div(b, STEPS)) & (lax.rem(a, STEPS) + lax.rem(b, STEPS) == STEPS - 1))
-    adjoint[...] = permute(back, plain)
+    adjoint[...] = turned - traces[width:width + 1, :] * slot_obs
     lax.fori_loop(1, peers, drain, 0)
 
 
-def wave_kernel(state, wb, ws, elem, live, cpl, out, u, x, xp, turned, faces, pick, rows_out, mixer):
+def wave_kernel(state, wb, ws, pick, live, mixer, out, u, x, xp, turned, faces, rows_out):
     fields, total, lanes = u.shape
     span = state.shape[1]
     count = span - 2 * HALO
@@ -224,11 +236,7 @@
         for grp in range(groups):
             put(grp, f, u[f, grp * TILE:(grp + 1) * TILE])
 
-    for i in range(mixer.shape[0]):
-        mixer[i] = jnp.full((SUB, lanes), cpl[i], jnp.float32)
     first, last = own // TILE, (own + count - 1) // TILE
-    ids = lax.broadcasted_iota(jnp.int32, pick.shape, 0) + (first * TILE - own)
-    pick[...] = jnp.where(ids == elem[...], live[...], 0.0)
     xp[...] = jnp.zeros(xp.shape, xp.dtype)
 
     def spread(grp):
@@ -333,7 +341,7 @@
     wide = -(-(width + 1) // 64) * 64
     f32, bf16 = jnp.float32, jnp.bfloat16
     square = pltpu.VMEM((slots, slots), bf16)
-    state, wb, ws, to_send, from_send, to_place, from_place, live = pl.pallas_call(
+    state, wb, ws, to_send, from_send, to_place, from_place, live, mixer, pick = pl.pallas_call(
         functools.partial(start_kernel, peers),
         out_shape=(
             pltpu.VMEM((fields + metric.shape[0] + 1, span, lanes), f32),
@@ -341,22 +349,25 @@
             pltpu.VMEM((3 * lanes, slots), bf16),
             square, square, square, square,
             pltpu.VMEM((1, slots), f32),
+            pltpu.VMEM((coupling.size, SUB, lanes), f32),
+            pltpu.VMEM((picked, slots), f32),
         ),
-        in_specs=[VM] * 7,
-        out_specs=[VM] * 8,
+        in_specs=[VM] * 9,
+        out_specs=[VM] * 10,
         scratch_shapes=[
             pltpu.VMEM((lanes, lanes), f32),
             pltpu.VMEM((lanes, slots), f32),
             pltpu.SemaphoreType.DMA((2,)),
             pltpu.SemaphoreType.DMA((2,)),
         ],
-        compiler_params=pltpu.CompilerParams(collective_id=0, has_side_effects=True),
+        compiler_params=pltpu.CompilerParams(collective_id=0, has_side_effects=True, vmem_limit_bytes=GRANT),
         name="start",
-    )(initial, metric, derivative, face_lift, rec_weight, shot_order.reshape(peers, slots), live_counts[None, :])
+    )(initial, metric, derivative, face_lift.transpose(1, 0, 2), rec_weight, shot_order.reshape(-1, lanes), live_counts[None, :],
+      rec_element[None, :], coupling.transpose(1, 0, 2))
     traces = pl.pallas_call(
         wave_kernel,
         out_shape=pltpu.VMEM((wide, slots), f32),
-        in_specs=[VM] * 5 + [pl.BlockSpec(memory_space=pltpu.SMEM)],
+        in_specs=[VM] * 6,
         out_specs=VM,
         scratch_shapes=[
             pltpu.VMEM((fields, total, lanes), f32),
@@ -364,12 +375,11 @@
             pltpu.VMEM((picked, 2 * lanes), bf16),
             pltpu.VMEM((kinds + 1, fields, total, lanes), f32),
             pltpu.VMEM((2, fields, total + 2 * GUARD, lanes), f32),
-            pltpu.VMEM((picked, slots), f32),
             pltpu.VMEM((STEPS + 1, 8, slots), f32),
-            pltpu.VMEM((coupling.size, SUB, lanes), f32),
         ],
+        compiler_params=pltpu.CompilerParams(vmem_limit_bytes=GRANT),
         name="waves",
-    )(vm(state), vm(wb), vm(ws), rec_element[None, :], vm(live), coupling.reshape(-1))
+    )(vm(state), vm(wb), vm(ws), vm(pick), vm(live), vm(mixer))
     residual, misfit, adjoint = pl.pallas_call(
         functools.partial(end_kernel, peers),
         out_shape=(
@@ -385,7 +395,7 @@
             pltpu.SemaphoreType.DMA((peers,)),
             pltpu.SemaphoreType.DMA((peers,)),
         ],
-        compiler_params=pltpu.CompilerParams(collective_id=1, has_side_effects=True),
+        compiler_params=pltpu.CompilerParams(collective_id=1, has_side_effects=True, vmem_limit_bytes=GRANT),
         name="finish",
     )(vm(traces), observed.T, vm(to_send), vm(from_send), vm(to_place), vm(from_place))
     return residual.T, misfit[0], adjoint.T

time: 51.5 us -> 58.9 us (1.14)
  local copies, waits for them, and re-layouts: 5.37 us -> 9.05 us
  Pallas kernels: 45.2 us -> 48.8 us
    unnamed x7 -> x23, local copies, waits for them, and re-layouts: 3.38 us -> 9.05 us
    pallas_call x1, Pallas kernels: 26.6 us -> 31.8 us  [shards(): pl.pallas_call(wave_kernel, out_shape=pltpu.VMEM((wide, slots), f32), in_...]
    reshape x2 -> x0, local copies, waits for them, and re-layouts: 1.99 us -> none  [the longest x1 1.33 us: shards(): shot_order.reshape(peers, slots)]
    pallas_call x1, Pallas kernels: 9.73 us -> 8.49 us  [shards(): pl.pallas_call(functools.partial(start_kernel, peers), out_shape=(pltpu.V...]
where the time goes in v2:
time: 58.9 us; the launch traced here: 58.5 us
  Pallas kernels  48.8 us (83%)
  local copies, waits for them, and re-layouts  9.05 us (15%)
  between operations  0.68 us (1%)
    pallas_call x1, Pallas kernels, shards(): pl.pallas_call(wave_kernel, out_shape=pltpu.VMEM((wide, slots), f32), in_...  31.8 us
    unnamed x23, local copies, waits for them, and re-layouts  9.05 us
    pallas_call x1, Pallas kernels, shards(): pl.pallas_call(functools.partial(start_kernel, peers), out_shape=(pltpu.V...  8.49 us
    pallas_call x1, Pallas kernels, shards(): pl.pallas_call(functools.partial(end_kernel, peers), out_shape=(pltpu.VME...  8.48 us

profile of v2, /device:TPU:0, one launch (start us, length us, event | category | flops | bytes accessed | tf_op | source)
XLA Modules:
  0.0 58.5 jit_solution(15426926700352429425)
XLA Ops:
  0.6 0.0 copy-start
  0.6 1.1 %copy-done = f32[9,125,128]{2,1,0:T(8,128)S(1)} copy-done((f32[9,125,128]{2,1,0:T(8,128)S(1)}, f32[9,125,128]{2,1,0:T(8,128)}, u32[]{:S(2)}) %copy-start) | copy-done | bytes 576024
  1.7 0.0 copy-start.1
  1.7 0.9 %copy-done.1 = f32[3,125,125]{2,1,0:T(8,128)S(1)} copy-done((f32[3,125,125]{2,1,0:T(8,128)S(1)}, f32[3,125,125]{2,1,0:T(8,128)}, u32[]{:S(2)}) %copy-start.1) | copy-done | bytes 187524
  2.6 0.0 copy-start.2
  2.6 0.9 %copy-done.2 = f32[125,256]{1,0:T(8,128)S(1)} copy-done((f32[125,256]{1,0:T(8,128)S(1)}, f32[125,256]{1,0:T(8,128)}, u32[]{:S(2)}) %copy-start.2) | copy-done | bytes 128024
  3.5 0.0 copy-start.3
  3.5 0.9 %copy-done.3 = f32[2,125,125]{2,0,1:T(2,128)S(1)} copy-done((f32[2,125,125]{2,0,1:T(2,128)S(1)}, f32[2,125,125]{2,0,1:T(2,128)}, u32[]{:S(2)}) %copy-start.3) | copy-done | bytes 125024
  4.4 0.0 copy-start.5
  4.4 0.7 %copy-done.5 = f32[3,9,9]{2,0,1:T(4,128)S(1)} copy-done((f32[3,9,9]{2,0,1:T(4,128)S(1)}, f32[3,9,9]{2,0,1:T(4,128)}, u32[]{:S(2)}) %copy-start.5) | copy-done | bytes 996
  5.2 0.0 copy-start.6
  5.2 0.7 %copy-done.6 = s32[4096]{0:T(1024)S(1)} copy-done((s32[4096]{0:T(1024)S(1)}, s32[4096]{0:T(1024)}, u32[]{:S(2)}) %copy-start.6) | copy-done | bytes 16408
  5.9 0.0 copy-start.7
  5.9 0.7 %copy-done.7 = f32[3,128]{1,0:T(4,128)S(1)} copy-done((f32[3,128]{1,0:T(4,128)S(1)}, f32[3,128]{1,0:T(4,128)}, u32[]{:S(2)}) %copy-start.7) | copy-done | bytes 1560
  6.6 0.0 copy-start.8
  6.6 0.7 %copy-done.8 = s32[256]{0:T(256)S(1)} copy-done((s32[256]{0:T(256)S(1)}, s32[256]{0:T(256)}, u32[]{:S(2)}) %copy-start.8) | copy-done | bytes 1048
  7.2 0.0 copy-start.9
  7.2 0.7 %copy-done.9 = s32[16]{0:T(128)S(1)} copy-done((s32[16]{0:T(128)S(1)}, s32[16]{0:T(128)}, u32[]{:S(2)}) %copy-start.9) | copy-done | bytes 88
  7.9 8.5 %start.1 = (f32[13,160,128]{2,1,0:T(8,128)S(1)}, bf16[384,768]{1,0:T(8,128)(2,1)S(1)}, bf16[384,256]{1,0:T(8,128)(2,1)S(1)}, bf16[256,256]{1,0:T(8,128)(2,1)S(1)...) custom-call(f32[9,125,128]{2,1,0:T(8,128)S(1)} %copy-done, ...), custom_call_target="tpu_custom_call" | custom-call | tf_op jit(solution)/shard_map/start/pallas_call | solution.py:344
  16.4 0.0 copy-start.4
  16.4 31.8 %waves.1.traces = f32[64,256]{1,0:T(8,128)S(1)} custom-call(f32[13,160,128]{2,1,0:T(8,128)S(1)} %get-tuple-element.16.state, bf16[384,768]{1,0:T(8,128)(2,1)S(1)} %get-tuple-element.17.wb, bf16[384,256]{1,0:T(8,128)(2,1)S(1)} %get-tuple-element.18.ws, f32[144,256]{1,0:T(8,128)S(1)} %get-tuple-element.19.pick, f32[1,256]{1,0:T(1,128)S(1)} %get-tuple-element.20.live, ...), custom_call_target="tpu_custom_call" | custom-call | tf_op jit(solution)/shard_map/waves/pallas_call | solution.py:367
  48.2 0.0 copy-done.4
  48.2 8.5 %finish.1 = (f32[48,256]{1,0:T(8,128)S(1)}, f32[1,256]{1,0:T(1,128)S(1)}, f32[48,256]{1,0:T(8,128)S(1)}) custom-call(f32[64,256]{1,0:T(8,128)S(1)} %waves.1.traces, f32[48,256]{1,0:T(8,128)S(1)} %bitcast.13, bf16[256,256]{1,0:T(8,128)(2,1)S(1)} %get-tuple-element.22.to_send, bf16[256,256]{1,0:T(8,128)(2,1)S(1)} %get-tuple-element.23.from_send, ...), custom_call_target="tpu_custom_call" | custom-call | tf_op jit(solution)/shard_map/finish/pallas_call | solution.py:383
  56.7 0.6 %copy.16 = f32[256,48]{0,1:T(8,128)} copy(f32[256,48]{0,1:T(8,128)S(1)} %bitcast.10) | data formatting | bytes 98304
  57.3 0.6 copy.17
  57.9 0.6 %copy.18 = f32[256,48]{0,1:T(8,128)} copy(f32[256,48]{0,1:T(8,128)S(1)} %bitcast.9) | data formatting | bytes 98304
Async XLA Ops:
  0.6 1.1 %copy-start = (f32[9,125,128]{2,1,0:T(8,128)S(1)}, f32[9,125,128]{2,1,0:T(8,128)}, u32[]{:S(2)}) copy-start(f32[9,125,128]{2,1,0:T(8,128)} %initial.1) | copy-start | bytes 1728004
  1.7 0.9 %copy-start.1 = (f32[3,125,125]{2,1,0:T(8,128)S(1)}, f32[3,125,125]{2,1,0:T(8,128)}, u32[]{:S(2)}) copy-start(f32[3,125,125]{2,1,0:T(8,128)} %derivative.1) | copy-start | bytes 562504
  2.6 0.9 %copy-start.2 = (f32[125,256]{1,0:T(8,128)S(1)}, f32[125,256]{1,0:T(8,128)}, u32[]{:S(2)}) copy-start(f32[125,256]{1,0:T(8,128)} %weight_in.1) | copy-start | bytes 384004
  3.5 0.9 %copy-start.3 = (f32[2,125,125]{2,0,1:T(2,128)S(1)}, f32[2,125,125]{2,0,1:T(2,128)}, u32[]{:S(2)}) copy-start(f32[2,125,125]{2,0,1:T(2,128)} %param.13) | copy-start | bytes 375004
  4.4 0.7 %copy-start.5 = (f32[3,9,9]{2,0,1:T(4,128)S(1)}, f32[3,9,9]{2,0,1:T(4,128)}, u32[]{:S(2)}) copy-start(f32[3,9,9]{2,0,1:T(4,128)} %param.12) | copy-start | bytes 2920
  5.2 0.7 %copy-start.6 = (s32[4096]{0:T(1024)S(1)}, s32[4096]{0:T(1024)}, u32[]{:S(2)}) copy-start(s32[4096]{0:T(1024)} %param.18) | copy-start | bytes 49156
  5.9 0.7 %copy-start.7 = (f32[3,128]{1,0:T(4,128)S(1)}, f32[3,128]{1,0:T(4,128)}, u32[]{:S(2)}) copy-start(f32[3,128]{1,0:T(4,128)} %metric.1) | copy-start | bytes 4612
  6.6 0.7 %copy-start.8 = (s32[256]{0:T(256)S(1)}, s32[256]{0:T(256)}, u32[]{:S(2)}) copy-start(s32[256]{0:T(256)} %param.15) | copy-start | bytes 3076
  7.2 0.7 %copy-start.9 = (s32[16]{0:T(128)S(1)}, s32[16]{0:T(128)}, u32[]{:S(2)}) copy-start(s32[16]{0:T(128)} %param.17) | copy-start | bytes 196
  16.4 31.8 %copy-start.4 = (f32[256,48]{0,1:T(8,128)S(1)}, f32[256,48]{0,1:T(8,128)}, u32[]{:S(2)}) copy-start(f32[256,48]{0,1:T(8,128)} %param.19) | copy-start | bytes 147460

commit v3 on v2

--- a/solution.py
+++ b/solution.py
@@ -208,7 +208,7 @@
     lax.fori_loop(1, peers, drain, 0)
 
 
-def wave_kernel(state, wb, ws, pick, live, mixer, out, u, x, xp, turned, faces, rows_out):
+def wave_kernel(state, wb_in, ws_in, pick_in, live, mixer_in, out, u, x, xp, turned, faces, rows_out, pick, mixer, wb, ws, held):
     fields, total, lanes = u.shape
     span = state.shape[1]
     count = span - 2 * HALO
@@ -219,7 +219,11 @@
     groups = total // TILE
 
     def stored(f, r, n):
-        return state[f, r - margin:r - margin + n]
+        return held[f - fields, r - margin:r - margin + n]
+
+    wb[...] = wb_in[...]
+    ws[...] = ws_in[...]
+    held[...] = state[fields:]
 
     def put(grp, f, new):
         hi, lo = split(new)
@@ -238,6 +242,8 @@
 
     first, last = own // TILE, (own + count - 1) // TILE
     xp[...] = jnp.zeros(xp.shape, xp.dtype)
+    pick[...] = pick_in[...]
+    mixer[...] = mixer_in[...]
 
     def spread(grp):
         lhs = x[grp]
@@ -326,6 +332,10 @@
     return pltpu.with_memory_space_constraint(x, pltpu.VMEM)
 
 
+def far(x):
+    return pltpu.with_memory_space_constraint(x, pltpu.HBM)
+
+
 VM = pl.BlockSpec(memory_space=pltpu.VMEM)
 
 
@@ -362,8 +372,8 @@
         ],
         compiler_params=pltpu.CompilerParams(collective_id=0, has_side_effects=True, vmem_limit_bytes=GRANT),
         name="start",
-    )(initial, metric, derivative, face_lift.transpose(1, 0, 2), rec_weight, shot_order.reshape(-1, lanes), live_counts[None, :],
-      rec_element[None, :], coupling.transpose(1, 0, 2))
+    )(*(far(a) for a in (initial, metric, derivative, face_lift.transpose(1, 0, 2), rec_weight, shot_order.reshape(-1, lanes),
+                    live_counts[None, :], rec_element[None, :], coupling.transpose(1, 0, 2))))
     traces = pl.pallas_call(
         wave_kernel,
         out_shape=pltpu.VMEM((wide, slots), f32),
@@ -376,6 +386,11 @@
             pltpu.VMEM((kinds + 1, fields, total, lanes), f32),
             pltpu.VMEM((2, fields, total + 2 * GUARD, lanes), f32),
             pltpu.VMEM((STEPS + 1, 8, slots), f32),
+            pltpu.VMEM((picked, slots), f32),
+            pltpu.VMEM((coupling.size, SUB, lanes), f32),
+            pltpu.VMEM((3 * lanes, (kinds + 3) * lanes), bf16),
+            pltpu.VMEM((3 * lanes, slots), bf16),
+            pltpu.VMEM((kinds + 1, span, lanes), f32),
         ],
         compiler_params=pltpu.CompilerParams(vmem_limit_bytes=GRANT),
         name="waves",
@@ -397,7 +412,7 @@
         ],
         compiler_params=pltpu.CompilerParams(collective_id=1, has_side_effects=True, vmem_limit_bytes=GRANT),
         name="finish",
-    )(vm(traces), observed.T, vm(to_send), vm(from_send), vm(to_place), vm(from_place))
+    )(vm(traces), far(observed.T), vm(to_send), vm(from_send), vm(to_place), vm(from_place))
     return residual.T, misfit[0], adjoint.T
 
 

time: 58.9 us -> 47.1 us (0.80)
  local copies, waits for them, and re-layouts: 9.05 us -> 1.8 us
  Pallas kernels: 48.8 us -> 44.4 us
    unnamed x23 -> x3, local copies, waits for them, and re-layouts: 9.05 us -> 1.8 us
    pallas_call x1, Pallas kernels: 31.8 us -> 25.5 us  [shards(): pl.pallas_call(wave_kernel, out_shape=pltpu.VMEM((wide, slots), f32), in_...]
    pallas_call x1, Pallas kernels: 8.49 us -> 9.81 us  [shards(): pl.pallas_call(functools.partial(start_kernel, peers), out_shape=(pltpu.V...]
    pallas_call x1, Pallas kernels: 8.48 us -> 9.1 us  [shards(): pl.pallas_call(functools.partial(end_kernel, peers), out_shape=(pltpu.VME...]
where the time goes in v3:
time: 47.1 us; the launch traced here: 46.9 us
  Pallas kernels  44.4 us (94%)
  local copies, waits for them, and re-layouts  1.8 us (4%)
  between operations  0.65 us (1%)
    pallas_call x1, Pallas kernels, shards(): pl.pallas_call(wave_kernel, out_shape=pltpu.VMEM((wide, slots), f32), in_...  25.5 us
    pallas_call x1, Pallas kernels, shards(): pl.pallas_call(functools.partial(start_kernel, peers), out_shape=(pltpu.V...  9.81 us
    pallas_call x1, Pallas kernels, shards(): pl.pallas_call(functools.partial(end_kernel, peers), out_shape=(pltpu.VME...  9.1 us
    unnamed x3, local copies, waits for them, and re-layouts  1.8 us

profile of v3, /device:TPU:0, one launch (start us, length us, event | category | flops | bytes accessed | tf_op | source)
XLA Modules:
  0.0 46.9 jit_solution(13790959962587317280)
XLA Ops:
  0.6 9.8 %start.1 = (f32[13,160,128]{2,1,0:T(8,128)S(1)}, bf16[384,768]{1,0:T(8,128)(2,1)S(1)}, bf16[384,256]{1,0:T(8,128)(2,1)S(1)}, bf16[256,256]{1,0:T(8,128)(2,1)S(1)...) custom-call(f32[9,125,128]{2,1,0:T(8,128)} %initial.1, ...), custom_call_target="tpu_custom_call" | custom-call | tf_op jit(solution)/shard_map/start/pallas_call | solution.py:354
  10.4 25.5 %waves.1.traces = f32[64,256]{1,0:T(8,128)S(1)} custom-call(f32[13,160,128]{2,1,0:T(8,128)S(1)} %get-tuple-element.16.state, bf16[384,768]{1,0:T(8,128)(2,1)S(1)} %get-tuple-element.17.wb_in, bf16[384,256]{1,0:T(8,128)(2,1)S(1)} %get-tuple-element.18.ws_in, f32[144,256]{1,0:T(8,128)S(1)} %get-tuple-element.19.pick_in, f32[1,256]{1,0:T(1,128)S(1)} %get-tuple-element.20.live, ...), custom_call_target="tpu_custom_call" | custom-call | tf_op jit(solution)/shard_map/waves/pallas_call | solution.py:377
  36.0 9.1 %finish.1 = (f32[48,256]{1,0:T(8,128)S(1)}, f32[1,256]{1,0:T(1,128)S(1)}, f32[48,256]{1,0:T(8,128)S(1)}) custom-call(f32[64,256]{1,0:T(8,128)S(1)} %waves.1.traces, f32[48,256]{1,0:T(8,128)} %bitcast.13, bf16[256,256]{1,0:T(8,128)(2,1)S(1)} %get-tuple-element.22.to_send, bf16[256,256]{1,0:T(8,128)(2,1)S(1)} %get-tuple-element.23.from_send, ...), custom_call_target="tpu_custom_call" | custom-call | tf_op jit(solution)/shard_map/finish/pallas_call | solution.py:398
  45.1 0.6 %copy.16 = f32[256,48]{0,1:T(8,128)} copy(f32[256,48]{0,1:T(8,128)S(1)} %bitcast.10) | data formatting | bytes 98304
  45.7 0.6 %copy.17 = f32[256]{0:T(256)} copy(f32[256]{0:T(256)S(1)} %bitcast.11) | data formatting | bytes 2048
  46.3 0.6 %copy.18 = f32[256,48]{0,1:T(8,128)} copy(f32[256,48]{0,1:T(8,128)S(1)} %bitcast.9) | data formatting | bytes 98304

commit v4 on v3

--- a/solution.py
+++ b/solution.py
@@ -64,8 +64,12 @@
     me = lax.axis_index("mx")
     right, left = lax.rem(me + 1, peers), lax.rem(me + peers - 1, peers)
     barrier = pltpu.get_barrier_semaphore()
-    for side in (left, right):
-        pl.semaphore_signal(barrier, inc=1, device_id={"mx": side}, device_id_type=pl.DeviceIdType.MESH)
+    sides = ((me < peers - 1, right), (me > 0, left))
+    for there, side in sides:
+        @pl.when(there)
+        def hail():
+            pl.semaphore_signal(barrier, inc=1, device_id={"mx": side}, device_id_type=pl.DeviceIdType.MESH)
+
     pad[...] = zeros(lanes, lanes)
     for f in range(fields):
         pad[0:nodes, :] = initial[f]
@@ -73,7 +77,7 @@
     kinds = metric.shape[0]
     for k in range(kinds):
         state[fields + k, HALO:HALO + count] = jnp.broadcast_to(metric[k:k + 1, :], (lanes, count)).T
-    pl.semaphore_wait(barrier, 2)
+    pl.semaphore_wait(barrier, sum(there.astype(jnp.int32) for there, _ in sides))
     moved = fields + kinds
     copies = []
     for i, (side, at, to) in enumerate(((right, count, 0), (left, HALO, HALO + count))):
@@ -81,7 +85,16 @@
             src_ref=state.at[0:moved, at:at + HALO], dst_ref=state.at[0:moved, to:to + HALO],
             send_sem=send_sem.at[i], recv_sem=recv_sem.at[i],
             device_id={"mx": side}, device_id_type=pl.DeviceIdType.MESH))
-        copies[-1].start()
+
+    for (there, _), copy, edge in zip(sides, copies, (HALO + count, 0)):
+        @pl.when(there)
+        def send():
+            copy.start()
+
+        @pl.when(jnp.logical_not(there))
+        def blank():
+            state[0:moved, edge:edge + HALO] = zeros(moved, HALO, lanes)
+
     pad[...] = zeros(lanes, lanes)
     turns = derivative.shape[0]
 
@@ -147,18 +160,23 @@
             line = coupling[row, k:k + 1, :]
             for f in range(fields):
                 mixer[(k * fields + row) * fields + f] = jnp.broadcast_to(line[:, f:f + 1], (SUB, lanes))
-    for copy in copies:
-        copy.wait()
-
-
-def end_kernel(peers, traces, observed, to_send, from_send, to_place, from_place,
-               residual, misfit, adjoint, sent, got, send_sem, recv_sem):
+    for (there, _), out, back in zip(sides, copies, copies[::-1]):
+        @pl.when(there)
+        def finish():
+            out.wait_send()
+            back.wait_recv()
+
+
+def whole_kernel(peers, state, wb_in, ws_in, pick_in, live, mixer_in, observed, to_send, from_send, to_place, from_place,
+                 residual, misfit, adjoint, u, x, xp, turned, faces, rows_out, pick, mixer, wb, ws, held, traces,
+                 sent, got, send_sem, recv_sem):
     width, slots = observed.shape
     lanes = sent.shape[-1]
     wide = traces.shape[0]
     pair = slots // peers
     me = lax.axis_index("mx")
     barrier = greet(peers, me)
+    wave_part(state, wb_in, ws_in, pick_in, live, mixer_in, traces, u, x, xp, turned, faces, rows_out, pick, mixer, wb, ws, held)
     synth = traces[...].T
     packed = permute(to_send[...], synth)
     a = lax.broadcasted_iota(jnp.int32, (width, width), 0)
@@ -169,7 +187,7 @@
     sent[...] = row.reshape(peers, pair, lanes)
     pl.semaphore_wait(barrier, peers - 1)
 
-    turned = traces[width:width + 1, :] * permute(back, traces[0:width, :])
+    flipped = traces[width:width + 1, :] * permute(back, traces[0:width, :])
 
     def copy_to(off):
         dest = lax.rem(me + off, peers)
@@ -204,11 +222,11 @@
     residual[...] = res
     misfit[...] = 0.5 * jnp.sum(res * res, axis=0, keepdims=True)
     slot_obs = permute(from_send[...], arrived[:, wide:wide + width]).T
-    adjoint[...] = turned - traces[width:width + 1, :] * slot_obs
+    adjoint[...] = flipped - traces[width:width + 1, :] * slot_obs
     lax.fori_loop(1, peers, drain, 0)
 
 
-def wave_kernel(state, wb_in, ws_in, pick_in, live, mixer_in, out, u, x, xp, turned, faces, rows_out, pick, mixer, wb, ws, held):
+def wave_part(state, wb_in, ws_in, pick_in, live, mixer_in, out, u, x, xp, turned, faces, rows_out, pick, mixer, wb, ws, held):
     fields, total, lanes = u.shape
     span = state.shape[1]
     count = span - 2 * HALO
@@ -374,11 +392,15 @@
         name="start",
     )(*(far(a) for a in (initial, metric, derivative, face_lift.transpose(1, 0, 2), rec_weight, shot_order.reshape(-1, lanes),
                     live_counts[None, :], rec_element[None, :], coupling.transpose(1, 0, 2))))
-    traces = pl.pallas_call(
-        wave_kernel,
-        out_shape=pltpu.VMEM((wide, slots), f32),
-        in_specs=[VM] * 6,
-        out_specs=VM,
+    residual, misfit, adjoint = pl.pallas_call(
+        functools.partial(whole_kernel, peers),
+        out_shape=(
+            pltpu.VMEM((width, slots), f32),
+            pltpu.VMEM((1, slots), f32),
+            pltpu.VMEM((width, slots), f32),
+        ),
+        in_specs=[VM] * 11,
+        out_specs=[VM] * 3,
         scratch_shapes=[
             pltpu.VMEM((fields, total, lanes), f32),
             pltpu.VMEM((total // TILE, fields * TILE, 2 * lanes), bf16),
@@ -391,28 +413,15 @@
             pltpu.VMEM((3 * lanes, (kinds + 3) * lanes), bf16),
             pltpu.VMEM((3 * lanes, slots), bf16),
             pltpu.VMEM((kinds + 1, span, lanes), f32),
-        ],
-        compiler_params=pltpu.CompilerParams(vmem_limit_bytes=GRANT),
-        name="waves",
-    )(vm(state), vm(wb), vm(ws), vm(pick), vm(live), vm(mixer))
-    residual, misfit, adjoint = pl.pallas_call(
-        functools.partial(end_kernel, peers),
-        out_shape=(
-            pltpu.VMEM((width, slots), f32),
-            pltpu.VMEM((1, slots), f32),
-            pltpu.VMEM((width, slots), f32),
-        ),
-        in_specs=[VM] * 6,
-        out_specs=[VM] * 3,
-        scratch_shapes=[
+            pltpu.VMEM((wide, slots), f32),
             pltpu.VMEM((peers, slots // peers, lanes), f32),
             pltpu.VMEM((peers, slots // peers, lanes), f32),
             pltpu.SemaphoreType.DMA((peers,)),
             pltpu.SemaphoreType.DMA((peers,)),
         ],
         compiler_params=pltpu.CompilerParams(collective_id=1, has_side_effects=True, vmem_limit_bytes=GRANT),
-        name="finish",
-    )(vm(traces), far(observed.T), vm(to_send), vm(from_send), vm(to_place), vm(from_place))
+        name="whole",
+    )(vm(state), vm(wb), vm(ws), vm(pick), vm(live), vm(mixer), far(observed.T), vm(to_send), vm(from_send), vm(to_place), vm(from_place))
     return residual.T, misfit[0], adjoint.T
 
 

time: 47.1 us -> 44.5 us (0.945)
  Pallas kernels: 44.4 us -> 41.8 us
    pallas_call x1, Pallas kernels: 9.81 us -> 5.25 us  [shards(): pl.pallas_call(functools.partial(start_kernel, peers), out_shape=(pltpu.V...]
    pallas_call x2 -> x1, Pallas kernels: 34.6 us -> 36.6 us  [shards(): pl.pallas_call(functools.partial(whole_kernel, peers), out_shape=(pltpu.V...]
where the time goes in v4:
time: 44.5 us; the launch traced here: 44.3 us
  Pallas kernels  41.8 us (94%)
  local copies, waits for them, and re-layouts  1.8 us (4%)
  between operations  0.65 us (1%)
    pallas_call x1, Pallas kernels, shards(): pl.pallas_call(functools.partial(whole_kernel, peers), out_shape=(pltpu.V...  36.6 us
    pallas_call x1, Pallas kernels, shards(): pl.pallas_call(functools.partial(start_kernel, peers), out_shape=(pltpu.V...  5.25 us
    unnamed x3, local copies, waits for them, and re-layouts  1.8 us

profile of v4, /device:TPU:0, one launch (start us, length us, event | category | flops | bytes accessed | tf_op | source)
XLA Modules:
  0.0 44.3 jit_solution(10217849497838906392)
XLA Ops:
  0.6 5.3 %start.1 = (f32[13,160,128]{2,1,0:T(8,128)S(1)}, bf16[384,768]{1,0:T(8,128)(2,1)S(1)}, bf16[384,256]{1,0:T(8,128)(2,1)S(1)}, bf16[256,256]{1,0:T(8,128)(2,1)S(1)...) custom-call(f32[9,125,128]{2,1,0:T(8,128)} %initial.1, ...), custom_call_target="tpu_custom_call" | custom-call | tf_op jit(solution)/shard_map/start/pallas_call | solution.py:372
  5.9 36.6 %whole.1 = (f32[48,256]{1,0:T(8,128)S(1)}, f32[1,256]{1,0:T(1,128)S(1)}, f32[48,256]{1,0:T(8,128)S(1)}) custom-call(f32[13,160,128]{2,1,0:T(8,128)S(1)} %get-tuple-element.16.state, bf16[384,768]{1,0:T(8,128)(2,1)S(1)} %get-tuple-element.17.wb_in, bf16[384,256]{1,0:T(8,128)(2,1)S(1)} %get-tuple-element.18.ws_in, f32[144,256]{1,0:T(8,128)S(1)} %get-tuple-element.19.pick_in, ...), custom_call_target="tpu_custom_call" | custom-call | tf_op jit(solution)/shard_map/whole/pallas_call | solution.py:395
  42.5 0.6 %copy.16 = f32[256,48]{0,1:T(8,128)} copy(f32[256,48]{0,1:T(8,128)S(1)} %bitcast.10) | data formatting | bytes 98304
  43.1 0.6 %copy.17 = f32[256]{0:T(256)} copy(f32[256]{0:T(256)S(1)} %bitcast.11) | data formatting | bytes 2048
  43.7 0.6 %copy.18 = f32[256,48]{0,1:T(8,128)} copy(f32[256,48]{0,1:T(8,128)S(1)} %bitcast.9) | data formatting | bytes 98304

commit v5 on v4

--- a/solution.py
+++ b/solution.py
@@ -108,10 +108,10 @@
 
     for k in range(turns):
         weigh(k, derivative[k])
-    lower, upper = face_lift[:, 0, :], face_lift[:, 1, :]
-    weigh(turns, lower)
-    weigh(turns + 1, upper)
-    weigh(turns + 2, -(lower + upper))
+    below, above = face_lift[:, 0, :], face_lift[:, 1, :]
+    weigh(turns, below)
+    weigh(turns + 1, above)
+    weigh(turns + 2, -(below + above))
     padw[...] = zeros(lanes, slots)
     padw[0:nodes, :] = weight_in[...]
     hi, lo = split(padw[...])
@@ -131,10 +131,11 @@
     rank = jnp.where(mine, rank, -1.0)
     tall = lax.broadcasted_iota(jnp.int32, (slots, peers), 0)
     wide = lax.broadcasted_iota(jnp.int32, (slots, peers), 1)
-    repeat = ones_where(lax.div(tall, pair) == wide)
+    half, upper = pair // 2, slots // 2
+    repeat = ones_where(lax.div(lax.rem(tall, upper), half) == wide)
     rank_all = dot(repeat, rank.astype(jnp.bfloat16))
     slot_all = dot(repeat, slot.astype(jnp.float32).astype(jnp.bfloat16))
-    hit = rank_all == lax.rem(up, pair).astype(jnp.float32)
+    hit = rank_all == (lax.div(up, upper) * half + lax.rem(up, half)).astype(jnp.float32)
     send_slot = jnp.sum(jnp.where(hit, slot_all, 0.0), axis=1, keepdims=True)
     sends = jnp.where(send_slot == across.astype(jnp.float32), 1.0, 0.0)
     to_send[...] = sends.astype(jnp.bfloat16)
@@ -145,7 +146,7 @@
     from_peer = peer_ids == own_source
     seen = dot(ones_where(from_peer), tri) - 1.0
     own_rank = jnp.sum(jnp.where(from_peer, seen, 0.0), axis=0, keepdims=True)
-    place = own_source.astype(jnp.float32) * float(pair) + own_rank
+    place = own_source.astype(jnp.float32) * float(half) + own_rank + jnp.where(own_rank >= float(half), float(upper - half), 0.0)
     places = jnp.where(up.astype(jnp.float32) == place, 1.0, 0.0)
     to_place[...] = places.astype(jnp.bfloat16)
     from_place[...] = places.T.astype(jnp.bfloat16)
@@ -167,66 +168,87 @@
             back.wait_recv()
 
 
+def fold(rows, peers, lanes):
+    slots, wide = rows.shape
+    rows = jnp.concatenate([rows[:slots // 2], rows[slots // 2:]], axis=1)
+    return rows.reshape(peers, slots // 2 // peers, lanes)
+
+
+def unfold(block, wide):
+    rows = block.reshape(block.shape[0] * block.shape[1], block.shape[2])
+    return jnp.concatenate([rows[:, 0:wide], rows[:, wide:]], axis=0)
+
+
 def whole_kernel(peers, state, wb_in, ws_in, pick_in, live, mixer_in, observed, to_send, from_send, to_place, from_place,
-                 residual, misfit, adjoint, u, x, xp, turned, faces, rows_out, pick, mixer, wb, ws, held, traces,
+                 outs, u, x, xp, turned, faces, rows_out, pick, mixer, wb, ws, held, traces,
                  sent, got, send_sem, recv_sem):
     width, slots = observed.shape
+    residual, misfit, adjoint = outs.at[0:width], outs.at[2 * width:2 * width + 1], outs.at[width:2 * width]
     lanes = sent.shape[-1]
     wide = traces.shape[0]
-    pair = slots // peers
     me = lax.axis_index("mx")
     barrier = greet(peers, me)
-    wave_part(state, wb_in, ws_in, pick_in, live, mixer_in, traces, u, x, xp, turned, faces, rows_out, pick, mixer, wb, ws, held)
-    synth = traces[...].T
-    packed = permute(to_send[...], synth)
     a = lax.broadcasted_iota(jnp.int32, (width, width), 0)
     b = lax.broadcasted_iota(jnp.int32, (width, width), 1)
     back = ones_where((lax.div(a, STEPS) == lax.div(b, STEPS)) & (lax.rem(a, STEPS) + lax.rem(b, STEPS) == STEPS - 1))
-    obs = permute(to_place[...], permute(back, observed[...]).T)
-    row = jnp.concatenate([packed, obs, zeros(slots, lanes - wide - width)], axis=1)
-    sent[...] = row.reshape(peers, pair, lanes)
-    pl.semaphore_wait(barrier, peers - 1)
-
-    flipped = traces[width:width + 1, :] * permute(back, traces[0:width, :])
-
-    def copy_to(off):
-        dest = lax.rem(me + off, peers)
+    mirrored = jnp.concatenate([permute(back, observed[...]), zeros(wide - width, slots)], axis=0)
+    sent[0] = fold(permute(to_place[...], mirrored.T), peers, lanes)
+
+    def offset(i):
+        return 1 + lax.rem(i + peers // 2 - 1, peers - 1)
+
+    def copy_to(which, i):
+        dest = lax.rem(me + offset(i), peers)
         return pltpu.make_async_remote_copy(
-            src_ref=sent.at[dest], dst_ref=got.at[me], send_sem=send_sem.at[dest], recv_sem=recv_sem.at[me],
+            src_ref=sent.at[which, dest], dst_ref=got.at[which, me],
+            send_sem=send_sem.at[which, dest], recv_sem=recv_sem.at[which, me],
             device_id={"mx": dest}, device_id_type=pl.DeviceIdType.MESH)
 
-    def copy_from(off):
-        src = lax.rem(me - off + peers, peers)
+    def copy_from(which, i):
+        src = lax.rem(me - offset(i) + peers, peers)
         return pltpu.make_async_remote_copy(
-            src_ref=sent.at[src], dst_ref=got.at[src], send_sem=send_sem.at[src], recv_sem=recv_sem.at[src],
+            src_ref=sent.at[which, src], dst_ref=got.at[which, src],
+            send_sem=send_sem.at[which, src], recv_sem=recv_sem.at[which, src],
             device_id={"mx": src}, device_id_type=pl.DeviceIdType.MESH)
 
-    def begin(off, _):
-        copy_to(off).start()
+    def begin(which, i, _):
+        copy_to(which, i).start()
         return 0
 
-    def finish(off, _):
-        copy_from(off).wait_recv()
+    def finish(which, i, _):
+        copy_from(which, i).wait_recv()
         return 0
 
-    def drain(off, _):
-        copy_to(off).wait_send()
+    def drain(which, i, _):
+        copy_to(which, i).wait_send()
         return 0
 
-    lax.fori_loop(1, peers, begin, 0)
-    got[pl.ds(me, 1)] = sent[pl.ds(me, 1)]
-    lax.fori_loop(1, peers, finish, 0)
-    arrived = got[...].reshape(slots, lanes)
-    placed = permute(from_place[...], arrived[:, :wide]).T
+    def each(action, which):
+        lax.fori_loop(0, peers - 1, functools.partial(action, which), 0)
+
+    def between():
+        pl.semaphore_wait(barrier, peers - 1)
+        each(begin, 0)
+        got[0, pl.ds(me, 1)] = sent[0, pl.ds(me, 1)]
+
+    wave_part(between, state, wb_in, ws_in, pick_in, live, mixer_in, traces, u, x, xp, turned, faces, rows_out, pick, mixer, wb, ws, held)
+    sent[1] = fold(permute(to_send[...], traces[...].T), peers, lanes)
+    each(begin, 1)
+    got[1, pl.ds(me, 1)] = sent[1, pl.ds(me, 1)]
+    each(finish, 0)
+    slot_obs = permute(from_send[...], unfold(got[0], wide)).T
+    mine = traces[width:width + 1, :]
+    adjoint[...] = mine * (permute(back, traces[0:width, :]) - slot_obs[0:width])
+    each(drain, 0)
+    each(finish, 1)
+    placed = permute(from_place[...], unfold(got[1], wide)).T
     res = placed[width:width + 1] * (placed[:width] - observed[...])
     residual[...] = res
     misfit[...] = 0.5 * jnp.sum(res * res, axis=0, keepdims=True)
-    slot_obs = permute(from_send[...], arrived[:, wide:wide + width]).T
-    adjoint[...] = flipped - traces[width:width + 1, :] * slot_obs
-    lax.fori_loop(1, peers, drain, 0)
-
-
-def wave_part(state, wb_in, ws_in, pick_in, live, mixer_in, out, u, x, xp, turned, faces, rows_out, pick, mixer, wb, ws, held):
+    each(drain, 1)
+
+
+def wave_part(between, state, wb_in, ws_in, pick_in, live, mixer_in, out, u, x, xp, turned, faces, rows_out, pick, mixer, wb, ws, held):
     fields, total, lanes = u.shape
     span = state.shape[1]
     count = span - 2 * HALO
@@ -337,6 +359,7 @@
     for grp in range(AHEAD):
         spread(grp)
     lax.fori_loop(0, WIDE, functools.partial(step, tuple(range(groups)), AHEAD), 0)
+    between()
     lax.fori_loop(WIDE, STEPS, functools.partial(step, tuple(range(first, last + 1)), AHEAD - 1), 0)
     sample(STEPS)
     out[...] = zeros(*out.shape)
@@ -392,15 +415,13 @@
         name="start",
     )(*(far(a) for a in (initial, metric, derivative, face_lift.transpose(1, 0, 2), rec_weight, shot_order.reshape(-1, lanes),
                     live_counts[None, :], rec_element[None, :], coupling.transpose(1, 0, 2))))
-    residual, misfit, adjoint = pl.pallas_call(
+    out, = pl.pallas_call(
         functools.partial(whole_kernel, peers),
         out_shape=(
-            pltpu.VMEM((width, slots), f32),
-            pltpu.VMEM((1, slots), f32),
-            pltpu.VMEM((width, slots), f32),
+            pltpu.VMEM((2 * width + 8, slots), f32),
         ),
         in_specs=[VM] * 11,
-        out_specs=[VM] * 3,
+        out_specs=[VM],
         scratch_shapes=[
             pltpu.VMEM((fields, total, lanes), f32),
             pltpu.VMEM((total // TILE, fields * TILE, 2 * lanes), bf16),
@@ -414,15 +435,15 @@
             pltpu.VMEM((3 * lanes, slots), bf16),
             pltpu.VMEM((kinds + 1, span, lanes), f32),
             pltpu.VMEM((wide, slots), f32),
-            pltpu.VMEM((peers, slots // peers, lanes), f32),
-            pltpu.VMEM((peers, slots // peers, lanes), f32),
-            pltpu.SemaphoreType.DMA((peers,)),
-            pltpu.SemaphoreType.DMA((peers,)),
+            pltpu.VMEM((2, peers, slots // peers // 2, lanes), f32),
+            pltpu.VMEM((2, peers, slots // peers // 2, lanes), f32),
+            pltpu.SemaphoreType.DMA((2, peers)),
+            pltpu.SemaphoreType.DMA((2, peers)),
         ],
         compiler_params=pltpu.CompilerParams(collective_id=1, has_side_effects=True, vmem_limit_bytes=GRANT),
         name="whole",
     )(vm(state), vm(wb), vm(ws), vm(pick), vm(live), vm(mixer), far(observed.T), vm(to_send), vm(from_send), vm(to_place), vm(from_place))
-    return residual.T, misfit[0], adjoint.T
+    return out[:width].T, out[2 * width], out[width:2 * width].T
 
 
 def solution(mesh):

time: 44.5 us -> 44.3 us (level)
  local copies, waits for them, and re-layouts: 1.8 us -> 1.21 us
    unnamed x3 -> x0, local copies, waits for them, and re-layouts: 1.8 us -> none
    transpose x0 -> x1, local copies, waits for them, and re-layouts: none -> 0.64 us  [shards(): return (out[:width].T, out[2 * width], out[width:2 * width].T)]
    slice x0 -> x1, local copies, waits for them, and re-layouts: none -> 0.56 us  [shards(): return (out[:width].T, out[2 * width], out[width:2 * width].T)]
where the time goes in v5:
time: 44.3 us; the launch traced here: 44.1 us
  Pallas kernels  42.2 us (95%)
  local copies, waits for them, and re-layouts  1.21 us (3%)
  between operations  0.65 us (1%)
    pallas_call x1, Pallas kernels, shards(): pl.pallas_call(functools.partial(whole_kernel, peers), out_shape=(pltpu.V...  37 us
    pallas_call x1, Pallas kernels, shards(): pl.pallas_call(functools.partial(start_kernel, peers), out_shape=(pltpu.V...  5.25 us

profile of v5, /device:TPU:0, one launch (start us, length us, event | category | flops | bytes accessed | tf_op | source)
XLA Modules:
  0.0 44.1 jit_solution(7666580942691331093)
XLA Ops:
  0.6 5.3 %start.1 = (f32[13,160,128]{2,1,0:T(8,128)S(1)}, bf16[384,768]{1,0:T(8,128)(2,1)S(1)}, bf16[384,256]{1,0:T(8,128)(2,1)S(1)}, bf16[256,256]{1,0:T(8,128)(2,1)S(1)...) custom-call(f32[9,125,128]{2,1,0:T(8,128)} %initial.1, ...), custom_call_target="tpu_custom_call" | custom-call | tf_op jit(solution)/shard_map/start/pallas_call | solution.py:395
  5.9 37.0 %whole.1 = f32[104,256]{1,0:T(8,128)S(1)} custom-call(f32[13,160,128]{2,1,0:T(8,128)S(1)} %get-tuple-element.13.state, bf16[384,768]{1,0:T(8,128)(2,1)S(1)} %get-tuple-element.14.wb_in, bf16[384,256]{1,0:T(8,128)(2,1)S(1)} %get-tuple-element.15.ws_in, f32[144,256]{1,0:T(8,128)S(1)} %get-tuple-element.16.pick_in, f32[1,256]{1,0:T(1,128)S(1)} %get-tuple-element.17.live, ...), custom_call_target="tpu_custom_call" | custom-call | tf_op jit(solution)/shard_map/whole/pallas_call | solution.py:418
  42.9 0.6 %slice.10 = f32[1,256]{1,0:T(1,128)} slice(f32[104,256]{1,0:T(8,128)S(1)} %whole.1), slice={[96:97], [0:256]} | slice | bytes 2048 | tf_op jit(solution)/shard_map/slice | solution.py:446
  43.4 0.6 %slice_bitcast_fusion = (f32[256,48]{0,1:T(8,128)}, f32[256,48]{0,1:T(8,128)}) fusion(f32[104,256]{1,0:T(8,128)S(1)} %whole.1), kind=kLoop, calls=%fused_computation | loop fusion | bytes 196608 | tf_op jit(solution)/shard_map/transpose | solution.py:446

commit v6 on v5

--- a/solution.py
+++ b/solution.py
@@ -9,6 +9,7 @@
 STEPS = 12
 COMPS = 4
 HALO = 16
+REACH = 12
 GUARD = 8
 TILE = 16
 SUB = 8
@@ -53,8 +54,20 @@
     return barrier
 
 
-def start_kernel(peers, initial, metric, derivative, face_lift, weight_in, order, counts, elem, coupling,
-                 state, wb, ws, to_send, from_send, to_place, from_place, live, mixer, pick,
+def mirror(width):
+    a = lax.broadcasted_iota(jnp.int32, (width, width), 0)
+    b = lax.broadcasted_iota(jnp.int32, (width, width), 1)
+    return ones_where((lax.div(a, STEPS) == lax.div(b, STEPS)) & (lax.rem(a, STEPS) + lax.rem(b, STEPS) == STEPS - 1))
+
+
+def fold(rows, peers, lanes):
+    slots, wide = rows.shape
+    rows = jnp.concatenate([rows[:slots // 2], rows[slots // 2:]], axis=1)
+    return rows.reshape(peers, slots // 2 // peers, lanes)
+
+
+def start_kernel(peers, initial, metric, derivative, face_lift, weight_in, order, counts, elem, coupling, observed,
+                 state, wb, ws, to_send, from_send, told, from_place, live, mixer, pick,
                  pad, padw, send_sem, recv_sem):
     fields, nodes, count = initial.shape
     lanes = pad.shape[0]
@@ -80,20 +93,22 @@
     pl.semaphore_wait(barrier, sum(there.astype(jnp.int32) for there, _ in sides))
     moved = fields + kinds
     copies = []
-    for i, (side, at, to) in enumerate(((right, count, 0), (left, HALO, HALO + count))):
+    for i, (side, at, to) in enumerate(((right, HALO + count - REACH, HALO - REACH), (left, HALO, HALO + count))):
         copies.append(pltpu.make_async_remote_copy(
-            src_ref=state.at[0:moved, at:at + HALO], dst_ref=state.at[0:moved, to:to + HALO],
+            src_ref=state.at[0:moved, at:at + REACH], dst_ref=state.at[0:moved, to:to + REACH],
             send_sem=send_sem.at[i], recv_sem=recv_sem.at[i],
             device_id={"mx": side}, device_id_type=pl.DeviceIdType.MESH))
 
-    for (there, _), copy, edge in zip(sides, copies, (HALO + count, 0)):
+    state[0:moved, 0:HALO - REACH] = zeros(moved, HALO - REACH, lanes)
+    state[0:moved, HALO + count + REACH:] = zeros(moved, HALO - REACH, lanes)
+    for (there, _), copy, edge in zip(sides, copies, (HALO + count, HALO - REACH)):
         @pl.when(there)
         def send():
             copy.start()
 
         @pl.when(jnp.logical_not(there))
         def blank():
-            state[0:moved, edge:edge + HALO] = zeros(moved, HALO, lanes)
+            state[0:moved, edge:edge + REACH] = zeros(moved, REACH, lanes)
 
     pad[...] = zeros(lanes, lanes)
     turns = derivative.shape[0]
@@ -148,7 +163,9 @@
     own_rank = jnp.sum(jnp.where(from_peer, seen, 0.0), axis=0, keepdims=True)
     place = own_source.astype(jnp.float32) * float(half) + own_rank + jnp.where(own_rank >= float(half), float(upper - half), 0.0)
     places = jnp.where(up.astype(jnp.float32) == place, 1.0, 0.0)
-    to_place[...] = places.astype(jnp.bfloat16)
+    width = observed.shape[0]
+    mirrored = jnp.concatenate([permute(mirror(width), observed[...]), zeros(lanes // 2 - width, slots)], axis=0)
+    told[...] = fold(permute(places.astype(jnp.bfloat16), mirrored.T), peers, lanes)
     from_place[...] = places.T.astype(jnp.bfloat16)
     here = lax.broadcasted_iota(jnp.int32, (1, peers), 1) == me
     limit = jnp.sum(jnp.where(here, counts[...].astype(jnp.float32), 0.0), axis=1, keepdims=True)
@@ -168,18 +185,12 @@
             back.wait_recv()
 
 
-def fold(rows, peers, lanes):
-    slots, wide = rows.shape
-    rows = jnp.concatenate([rows[:slots // 2], rows[slots // 2:]], axis=1)
-    return rows.reshape(peers, slots // 2 // peers, lanes)
-
-
 def unfold(block, wide):
     rows = block.reshape(block.shape[0] * block.shape[1], block.shape[2])
     return jnp.concatenate([rows[:, 0:wide], rows[:, wide:]], axis=0)
 
 
-def whole_kernel(peers, state, wb_in, ws_in, pick_in, live, mixer_in, observed, to_send, from_send, to_place, from_place,
+def whole_kernel(peers, state, wb_in, ws_in, pick_in, live, mixer_in, observed, to_send, from_send, told, from_place,
                  outs, u, x, xp, turned, faces, rows_out, pick, mixer, wb, ws, held, traces,
                  sent, got, send_sem, recv_sem):
     width, slots = observed.shape
@@ -188,11 +199,8 @@
     wide = traces.shape[0]
     me = lax.axis_index("mx")
     barrier = greet(peers, me)
-    a = lax.broadcasted_iota(jnp.int32, (width, width), 0)
-    b = lax.broadcasted_iota(jnp.int32, (width, width), 1)
-    back = ones_where((lax.div(a, STEPS) == lax.div(b, STEPS)) & (lax.rem(a, STEPS) + lax.rem(b, STEPS) == STEPS - 1))
-    mirrored = jnp.concatenate([permute(back, observed[...]), zeros(wide - width, slots)], axis=0)
-    sent[0] = fold(permute(to_place[...], mirrored.T), peers, lanes)
+    sent[0] = told[...]
+    back = mirror(width)
 
     def offset(i):
         return 1 + lax.rem(i + peers // 2 - 1, peers - 1)
@@ -392,18 +400,18 @@
     wide = -(-(width + 1) // 64) * 64
     f32, bf16 = jnp.float32, jnp.bfloat16
     square = pltpu.VMEM((slots, slots), bf16)
-    state, wb, ws, to_send, from_send, to_place, from_place, live, mixer, pick = pl.pallas_call(
+    state, wb, ws, to_send, from_send, told, from_place, live, mixer, pick = pl.pallas_call(
         functools.partial(start_kernel, peers),
         out_shape=(
             pltpu.VMEM((fields + metric.shape[0] + 1, span, lanes), f32),
             pltpu.VMEM((3 * lanes, (kinds + 3) * lanes), bf16),
             pltpu.VMEM((3 * lanes, slots), bf16),
-            square, square, square, square,
+            square, square, pltpu.VMEM((peers, slots // peers // 2, lanes), f32), square,
             pltpu.VMEM((1, slots), f32),
             pltpu.VMEM((coupling.size, SUB, lanes), f32),
             pltpu.VMEM((picked, slots), f32),
         ),
-        in_specs=[VM] * 9,
+        in_specs=[VM] * 10,
         out_specs=[VM] * 10,
         scratch_shapes=[
             pltpu.VMEM((lanes, lanes), f32),
@@ -414,7 +422,7 @@
         compiler_params=pltpu.CompilerParams(collective_id=0, has_side_effects=True, vmem_limit_bytes=GRANT),
         name="start",
     )(*(far(a) for a in (initial, metric, derivative, face_lift.transpose(1, 0, 2), rec_weight, shot_order.reshape(-1, lanes),
-                    live_counts[None, :], rec_element[None, :], coupling.transpose(1, 0, 2))))
+                    live_counts[None, :], rec_element[None, :], coupling.transpose(1, 0, 2), observed.T)))
     out, = pl.pallas_call(
         functools.partial(whole_kernel, peers),
         out_shape=(
@@ -442,7 +450,7 @@
         ],
         compiler_params=pltpu.CompilerParams(collective_id=1, has_side_effects=True, vmem_limit_bytes=GRANT),
         name="whole",
-    )(vm(state), vm(wb), vm(ws), vm(pick), vm(live), vm(mixer), far(observed.T), vm(to_send), vm(from_send), vm(to_place), vm(from_place))
+    )(vm(state), vm(wb), vm(ws), vm(pick), vm(live), vm(mixer), far(observed.T), vm(to_send), vm(from_send), vm(told), vm(from_place))
     return out[:width].T, out[2 * width], out[width:2 * width].T
 
 

time: 44.3 us -> 43.6 us (0.984)
  Pallas kernels: 42.2 us -> 41.5 us
    pallas_call x1, Pallas kernels: 37 us -> 36.3 us  [shards(): pl.pallas_call(functools.partial(whole_kernel, peers), out_shape=(pltpu.V...]
where the time goes in v6:
time: 43.6 us; the launch traced here: 43.4 us
  Pallas kernels  41.5 us (95%)
  local copies, waits for them, and re-layouts  1.21 us (3%)
  between operations  0.65 us (1%)
    pallas_call x1, Pallas kernels, shards(): pl.pallas_call(functools.partial(whole_kernel, peers), out_shape=(pltpu.V...  36.3 us
    pallas_call x1, Pallas kernels, shards(): pl.pallas_call(functools.partial(start_kernel, peers), out_shape=(pltpu.V...  5.22 us

profile of v6, /device:TPU:0, one launch (start us, length us, event | category | flops | bytes accessed | tf_op | source)
XLA Modules:
  0.0 43.4 jit_solution(15805187614607600667)
XLA Ops:
  0.6 5.2 %start.1 = (f32[13,160,128]{2,1,0:T(8,128)S(1)}, bf16[384,768]{1,0:T(8,128)(2,1)S(1)}, bf16[384,256]{1,0:T(8,128)(2,1)S(1)}, bf16[256,256]{1,0:T(8,128)(2,1)S(1)...) custom-call(f32[9,125,128]{2,1,0:T(8,128)} %initial.1, ...), custom_call_target="tpu_custom_call" | custom-call | tf_op jit(solution)/shard_map/start/pallas_call | solution.py:403
  5.9 36.3 %whole.1 = f32[104,256]{1,0:T(8,128)S(1)} custom-call(f32[13,160,128]{2,1,0:T(8,128)S(1)} %get-tuple-element.13.state, bf16[384,768]{1,0:T(8,128)(2,1)S(1)} %get-tuple-element.14.wb_in, bf16[384,256]{1,0:T(8,128)(2,1)S(1)} %get-tuple-element.15.ws_in, f32[144,256]{1,0:T(8,128)S(1)} %get-tuple-element.16.pick_in, f32[1,256]{1,0:T(1,128)S(1)} %get-tuple-element.17.live, ...), custom_call_target="tpu_custom_call" | custom-call | tf_op jit(solution)/shard_map/whole/pallas_call | solution.py:426
  42.2 0.6 %slice.10 = f32[1,256]{1,0:T(1,128)} slice(f32[104,256]{1,0:T(8,128)S(1)} %whole.1), slice={[96:97], [0:256]} | slice | bytes 2048 | tf_op jit(solution)/shard_map/slice | solution.py:454
  42.7 0.6 %slice_bitcast_fusion = (f32[256,48]{0,1:T(8,128)}, f32[256,48]{0,1:T(8,128)}) fusion(f32[104,256]{1,0:T(8,128)S(1)} %whole.1), kind=kLoop, calls=%fused_computation | loop fusion | bytes 196608 | tf_op jit(solution)/shard_map/transpose | solution.py:454

commit v7 on v6

--- a/solution.py
+++ b/solution.py
@@ -67,7 +67,7 @@
 
 
 def start_kernel(peers, initial, metric, derivative, face_lift, weight_in, order, counts, elem, coupling, observed,
-                 state, wb, ws, to_send, from_send, told, from_place, live, mixer, pick,
+                 state, wb, ws, to_send, from_send, told, from_place, live, mixer, pick, kept,
                  pad, padw, send_sem, recv_sem):
     fields, nodes, count = initial.shape
     lanes = pad.shape[0]
@@ -164,6 +164,7 @@
     place = own_source.astype(jnp.float32) * float(half) + own_rank + jnp.where(own_rank >= float(half), float(upper - half), 0.0)
     places = jnp.where(up.astype(jnp.float32) == place, 1.0, 0.0)
     width = observed.shape[0]
+    kept[...] = observed[...]
     mirrored = jnp.concatenate([permute(mirror(width), observed[...]), zeros(lanes // 2 - width, slots)], axis=0)
     told[...] = fold(permute(places.astype(jnp.bfloat16), mirrored.T), peers, lanes)
     from_place[...] = places.T.astype(jnp.bfloat16)
@@ -400,7 +401,7 @@
     wide = -(-(width + 1) // 64) * 64
     f32, bf16 = jnp.float32, jnp.bfloat16
     square = pltpu.VMEM((slots, slots), bf16)
-    state, wb, ws, to_send, from_send, told, from_place, live, mixer, pick = pl.pallas_call(
+    state, wb, ws, to_send, from_send, told, from_place, live, mixer, pick, kept = pl.pallas_call(
         functools.partial(start_kernel, peers),
         out_shape=(
             pltpu.VMEM((fields + metric.shape[0] + 1, span, lanes), f32),
@@ -410,9 +411,10 @@
             pltpu.VMEM((1, slots), f32),
             pltpu.VMEM((coupling.size, SUB, lanes), f32),
             pltpu.VMEM((picked, slots), f32),
+            pltpu.VMEM((width, slots), f32),
         ),
         in_specs=[VM] * 10,
-        out_specs=[VM] * 10,
+        out_specs=[VM] * 11,
         scratch_shapes=[
             pltpu.VMEM((lanes, lanes), f32),
             pltpu.VMEM((lanes, slots), f32),
@@ -450,7 +452,7 @@
         ],
         compiler_params=pltpu.CompilerParams(collective_id=1, has_side_effects=True, vmem_limit_bytes=GRANT),
         name="whole",
-    )(vm(state), vm(wb), vm(ws), vm(pick), vm(live), vm(mixer), far(observed.T), vm(to_send), vm(from_send), vm(told), vm(from_place))
+    )(vm(state), vm(wb), vm(ws), vm(pick), vm(live), vm(mixer), vm(kept), vm(to_send), vm(from_send), vm(told), vm(from_place))
     return out[:width].T, out[2 * width], out[width:2 * width].T
 
 

time: 43.6 us -> 43 us (0.986)
  Pallas kernels: 41.5 us -> 41 us
    pallas_call x1, Pallas kernels: 36.3 us -> 35.8 us  [shards(): pl.pallas_call(functools.partial(whole_kernel, peers), out_shape=(pltpu.V...]
where the time goes in v7:
time: 43 us; the launch traced here: 42.9 us
  Pallas kernels  41 us (95%)
  local copies, waits for them, and re-layouts  1.21 us (3%)
  between operations  0.65 us (2%)
    pallas_call x1, Pallas kernels, shards(): pl.pallas_call(functools.partial(whole_kernel, peers), out_shape=(pltpu.V...  35.8 us
    pallas_call x1, Pallas kernels, shards(): pl.pallas_call(functools.partial(start_kernel, peers), out_shape=(pltpu.V...  5.21 us

profile of v7, /device:TPU:0, one launch (start us, length us, event | category | flops | bytes accessed | tf_op | source)
XLA Modules:
  0.0 42.9 jit_solution(8606156454903155717)
XLA Ops:
  0.6 5.2 %start.1 = (f32[13,160,128]{2,1,0:T(8,128)S(1)}, bf16[384,768]{1,0:T(8,128)(2,1)S(1)}, bf16[384,256]{1,0:T(8,128)(2,1)S(1)}, bf16[256,256]{1,0:T(8,128)(2,1)S(1)...) custom-call(f32[9,125,128]{2,1,0:T(8,128)} %initial.1, ...), custom_call_target="tpu_custom_call" | custom-call | tf_op jit(solution)/shard_map/start/pallas_call | solution.py:404
  5.9 35.8 %whole.1 = f32[104,256]{1,0:T(8,128)S(1)} custom-call(f32[13,160,128]{2,1,0:T(8,128)S(1)} %get-tuple-element.14.state, bf16[384,768]{1,0:T(8,128)(2,1)S(1)} %get-tuple-element.15.wb_in, bf16[384,256]{1,0:T(8,128)(2,1)S(1)} %get-tuple-element.16.ws_in, f32[144,256]{1,0:T(8,128)S(1)} %get-tuple-element.17.pick_in, f32[1,256]{1,0:T(1,128)S(1)} %get-tuple-element.18.live, ...), custom_call_target="tpu_custom_call" | custom-call | tf_op jit(solution)/shard_map/whole/pallas_call | solution.py:428
  41.7 0.6 %slice.10 = f32[1,256]{1,0:T(1,128)} slice(f32[104,256]{1,0:T(8,128)S(1)} %whole.1), slice={[96:97], [0:256]} | slice | bytes 2048 | tf_op jit(solution)/shard_map/slice | solution.py:456
  42.2 0.6 %slice_bitcast_fusion = (f32[256,48]{0,1:T(8,128)}, f32[256,48]{0,1:T(8,128)}) fusion(f32[104,256]{1,0:T(8,128)S(1)} %whole.1), kind=kLoop, calls=%fused_computation | loop fusion | bytes 196608 | tf_op jit(solution)/shard_map/transpose | solution.py:456
